TPU v7x, 32 devices: a whole 2x2x4 slice. The times are simulated.
32 devices in a mesh: batch: 2 (over x), seq: 16 (over z, y, core).
Axes of the slice: x: 2, y: 2, z: 4, core: 2. Of those that a mesh axis runs over, the one named last changes fastest.
Arguments:
- hidden: bfloat16 [32, 4, 7168], P('batch'), parts along dimension 0
- cache_lens: int32 [32], P('batch'), parts along dimension 0
- c_kv: bfloat16 [32, 16384, 512], P('batch', 'seq'), parts along dimension 0
- k_r: bfloat16 [32, 16384, 64], P('batch', 'seq'), parts along dimension 0
- w_uq: bfloat16 [7168, 128, 128], P(None, 'seq')
- w_qr: bfloat16 [7168, 128, 64], P(None, 'seq')
- w_uk: bfloat16 [128, 128, 512], P('seq')
- w_uv: bfloat16 [128, 512, 128], P('seq')
- w_o: bfloat16 [128, 128, 7168], P('seq')
Outputs:
- output: bfloat16 [32, 4, 7168], P('batch'), parts along dimension 0
There are 2 independent parts. A program takes and returns all parts, laid end to end along the dimension named above; an argument that names none is the same for every part.
All inputs are finite; a program needn't handle non-finite values.
Results may differ from a plain program's by a relative error of at most 0.00665442.
Values are sent between devices in bfloat16 or wider.
A program may use at most 1 GiB of HBM per device.

v0:
```python
import jax
import jax.numpy as jnp
from jax import lax
from jax.sharding import PartitionSpec as P

MASK_FILL = -1e30


def solution(mesh):
    def local_step(hidden, cache_lens, c_kv, k_r, w_uq, w_qr, w_uk, w_uv, w_o):
        score_scale = (w_uq.shape[2] + w_qr.shape[2]) ** -0.5
        q_nope = jnp.einsum("cre,eil->cril", hidden, w_uq, preferred_element_type=jnp.float32).astype(jnp.bfloat16)
        q_rope = jnp.einsum("cre,eis->cris", hidden, w_qr, preferred_element_type=jnp.float32).astype(jnp.bfloat16)
        q_lat = jnp.einsum("bqhk,hkc->bqhc", q_nope, w_uk, preferred_element_type=jnp.float32).astype(jnp.bfloat16)
        lat_all = lax.all_gather(q_lat, "seq", axis=2, tiled=True)
        rope_all = lax.all_gather(q_rope, "seq", axis=2, tiled=True)
        local_len = c_kv.shape[1]
        positions = lax.axis_index("seq") * local_len + jnp.arange(local_len)
        limits = cache_lens[:, None] + jnp.arange(hidden.shape[1])[None, :]
        visible = positions[None, None, None, :] <= limits[:, :, None, None]
        scores = (jnp.einsum("bqhc,btc->bqht", lat_all, c_kv, preferred_element_type=jnp.float32)
                  + jnp.einsum("bqhr,btr->bqht", rope_all, k_r, preferred_element_type=jnp.float32)) * score_scale
        scores = jnp.where(visible, scores, MASK_FILL)
        local_max = jnp.max(scores, axis=-1)
        weights = jnp.exp(scores - local_max[..., None])
        local_sum = jnp.sum(weights, axis=-1)
        o_part = jnp.einsum("bqht,btc->bqhc", weights.astype(jnp.bfloat16), c_kv, preferred_element_type=jnp.float32)
        global_max = lax.pmax(local_max, "seq")
        rescale = jnp.exp(local_max - global_max)
        o_sum = lax.psum_scatter(o_part * rescale[..., None], "seq", scatter_dimension=2, tiled=True)
        l_sum = lax.psum_scatter(local_sum * rescale, "seq", scatter_dimension=2, tiled=True)
        o_lat = (o_sum / l_sum[..., None]).astype(jnp.bfloat16)
        o_val = jnp.einsum("bqhc,hcv->bqhv", o_lat, w_uv, preferred_element_type=jnp.float32).astype(jnp.bfloat16)
        y_part = jnp.einsum("criw,iwe->cre", o_val, w_o, preferred_element_type=jnp.float32)
        y_sum = lax.psum(y_part, "seq")
        return (hidden.astype(jnp.float32) + y_sum).astype(jnp.bfloat16)

    specs_in = (P("batch", None, None), P("batch"), P("batch", "seq", None), P("batch", "seq", None),
                P(None, "seq", None), P(None, "seq", None), P("seq", None, None), P("seq", None, None),
                P("seq", None, None))
    return jax.shard_map(local_step, mesh=mesh, in_specs=specs_in, out_specs=P("batch", None, None), check_vma=False)
```

profile of v0, /device:TPU:1, one launch (start us, length us, event | category | flops | bytes accessed | tf_op | source)
XLA Modules:
  0.0 546.6 jit_solution(521670691270134943)
XLA Ops:
  6.5 0.0 copy-start
  6.5 0.0 copy-start.2
  6.5 0.0 all-gather.3.cloned.1.call-start
  6.5 0.0 copy-start.4
  6.5 8.3 %fusion.30 = bf16[16,4,8,128]{3,0,2,1:T(8,128)(2,1)S(1)} fusion(bf16[7168,8,128]{2,1,0:T(8,128)(2,1)} %param.13, bf16[16,4,7168,1]{2,1,0,3:T(4,128)(2,1)} %bitcast.57), kind=kOutput, calls=%fused_computation.25 | convolution fusion | flops 939589632 | bytes 15728640 | tf_op jit(solution)/shard_map/cre,eil->cril/dot_general | solution.py:12
  14.8 0.0 copy-done.2
  14.8 1.1 fusion.26
  15.9 0.0 all-gather.3.cloned.1.call-update
  15.9 0.0 all-gather.5.cloned.1.call-start
  16.0 7.6 %fusion.27 = bf16[16,4,8,64]{3,0,2,1:T(8,128)(2,1)} fusion(bf16[7168,8,64]{0,2,1:T(8,128)(2,1)} %param.14, bf16[16,4,7168,1]{2,1,0,3:T(4,128)(2,1)} %bitcast.58), kind=kOutput, calls=%fused_computation.24 | convolution fusion | flops 469794816 | bytes 8323072 | tf_op jit(solution)/shard_map/cre,eis->cris/dot_general | solution.py:13
  23.6 0.0 all-gather.5.cloned.1.call-update
  23.6 0.2 reduce-scatter.2.cloned.1.call-start
  23.9 0.0 copy-done.4
  23.9 0.1 iota_add_fusion
  24.0 0.1 broadcast_compare_fusion
  24.1 69.0 %all-gather.3.cloned.1.call-done = bf16[16,4,128,512]{3,0,1,2:T(8,128)(2,1)} async-done(((bf16[16,4,8,512]{3,0,1,2:T(8,128)(2,1)}), bf16[16,4,128,512]{3,0,1,2:T(8,128)(2,1)}) %all-gather.3.cloned.1.call-update) | async-done | bytes 8388624 | tf_op jit(solution)/shard_map/all_gather | solution.py:15
  93.1 34.4 %fusion.5 = f32[16,4,128,1024]{3,2,1,0:T(8,128)} fusion(bf16[16,1024,512]{2,1,0:T(8,128)(2,1)} %param.11, bf16[16,4,128,512]{3,0,1,2:T(8,128)(2,1)} %all-gather.3.cloned.1.call-done), kind=kOutput, calls=%fused_computation.6 | convolution fusion | flops 8589934592 | bytes 58720256 | tf_op jit(solution)/shard_map/bqhc,btc->bqht/dot_general | solution.py:21
  127.5 7.7 %all-gather.5.cloned.1.call-done = bf16[16,4,128,64]{3,0,2,1:T(8,128)(2,1)} async-done(((bf16[16,4,8,64]{3,0,2,1:T(8,128)(2,1)}), bf16[16,4,128,64]{3,0,2,1:T(8,128)(2,1)}) %all-gather.5.cloned.1.call-update) | async-done | bytes 1048592 | tf_op jit(solution)/shard_map/all_gather | solution.py:16
  135.2 0.0 copy-done
  135.2 23.3 %fusion.43 = (f32[16,4,128]{2,1,0:T(4,128)S(1)}, f32[16,4,128,1024]{3,2,1,0:T(8,128)}) fusion(f32[16,4,128,1024]{3,2,1,0:T(8,128)} %fusion.5, bf16[16,1024,64]{1,2,0:T(8,128)(2,1)S(1)} %copy-done, bf16[16,4,128,64]{3,0,2,1:T(8,128)(2,1)} %all-gather.5.cloned.1.call-done, pred[16,4,1024]{2,1,0:T(4,128)(4,1)S(1)} %broadcast_compare_fusion), kind=kOutput, calls=%fused_computation.41 | convolution fusion | flops 1107288064 | bytes 70352896 | tf_op jit(solution)/shard_map/bqhr,btr->bqht/dot_general | solution.py:22
  158.6 54.4 %pmax.7 = f32[16,4,128]{2,1,0:T(4,128)S(1)} all-reduce(f32[16,4,128]{2,1,0:T(4,128)S(1)} %get-tuple-element.7), channel_id=1, replica_groups=mesh['batch'=2,'seq'=16] {'seq'}, use_global_device_ids=true, to_apply=%region_1.2 | all-reduce | flops 8192 | bytes 65536 | tf_op jit(solution)/shard_map/pmax | solution.py:28
  213.0 14.2 %fusion = f32[16,4,128]{2,1,0:T(4,128)S(1)} fusion(f32[16,4,128,1024]{3,2,1,0:T(8,128)} %get-tuple-element.8, f32[16,4,128]{2,1,0:T(4,128)S(1)} %get-tuple-element.7), kind=kLoop, calls=%fused_computation.2 | loop fusion | flops 16769024 | bytes 33619968 | tf_op jit(solution)/shard_map/reduce_sum | solution.py:26
  227.1 25.7 %fusion.13 = f32[16,4,128,512]{3,2,1,0:T(8,128)} fusion(bf16[16,1024,512]{2,1,0:T(8,128)(2,1)} %param.11, f32[16,4,128,1024]{3,2,1,0:T(8,128)} %get-tuple-element.8, f32[16,4,128]{2,1,0:T(4,128)S(1)} %get-tuple-element.7, f32[16,4,128]{2,1,0:T(4,128)S(1)} %bitcast.63), kind=kOutput, calls=%fused_computation.14 | convolution fusion | flops 8610906112 | bytes 67174400 | tf_op jit(solution)/shard_map/bqht,btc->bqhc/dot_general | solution.py:27
  252.8 0.0 copy-start.5
  252.8 0.0 reduce-scatter.2.cloned.1.call-update
  252.8 0.0 copy-start.3
  252.9 0.0 all-reduce.3.cloned.1.call-start
  252.9 0.6 copy-done.5
  253.5 0.6 dynamic-slice
  254.7 0.2 copy.35
  254.9 62.0 %all-reduce = f32[16,4,128]{0,1,2:T(4,128)S(1)} all-reduce(f32[16,4,128]{0,1,2:T(4,128)S(1)} %copy.35), channel_id=3, replica_groups=mesh['batch'=2,'seq'=16] {'seq'}, use_global_device_ids=true, to_apply=%region_4.5.clone | all-reduce | flops 8192 | bytes 65536
  316.9 0.7 copy.36
  317.6 112.7 %reduce-scatter.2.cloned.1.call-done = f32[16,4,8,512]{3,2,1,0:T(8,128)} async-done(((f32[16,4,128,512]{3,2,1,0:T(8,128)}), f32[16,4,8,512]{3,2,1,0:T(8,128)}) %reduce-scatter.2.cloned.1.call-update) | async-done | bytes 1048592 | tf_op jit(solution)/shard_map/reduce_scatter | solution.py:30
  430.3 0.0 copy-start.1
  430.3 1.5 divide_convert_fusion
  431.8 8.4 %fusion.19 = f32[16,4,7168]{2,0,1:T(8,128)} fusion(bf16[8,128,7168]{2,1,0:T(8,128)(2,1)} %param.17, bf16[8,512,128]{2,1,0:T(8,128)(2,1)} %param.16, bf16[16,4,8,512]{3,2,1,0:T(8,128)(2,1)S(1)} %divide_convert_fusion), kind=kOutput, calls=%fused_computation.16 | convolution fusion | flops 1006698496 | bytes 18087936 | tf_op jit(solution)/shard_map/criw,iwe->cre/dot_general | solution.py:34
  440.2 0.0 all-reduce.3.cloned.1.call-update
  440.2 96.4 %all-reduce.3.cloned.1.call-done = f32[16,4,7168]{2,0,1:T(8,128)} async-done(((f32[16,4,7168]{2,0,1:T(8,128)}), f32[16,4,7168]{2,0,1:T(8,128)}) %all-reduce.3.cloned.1.call-update) | async-done | bytes 1835024 | tf_op jit(solution)/shard_map/psum | solution.py:35
  536.6 0.0 copy-done.3
  536.6 1.8 add_convert_fusion
  538.4 1.6 copy.38
  540.1 0.0 copy-done.1
  (3 shorter events, 0.0 us)
Async XLA Ops:
  6.5 128.7 %copy-start = (bf16[16,1024,64]{1,2,0:T(8,128)(2,1)S(1)}, bf16[16,1024,64]{1,2,0:T(8,128)(2,1)}, u32[]{:S(2)}) copy-start(bf16[16,1024,64]{1,2,0:T(8,128)(2,1)} %param.12) | copy-start | bytes 6291460
  6.5 8.3 %copy-start.2 = (bf16[8,128,512]{2,1,0:T(8,128)(2,1)S(1)}, bf16[8,128,512]{2,1,0:T(8,128)(2,1)}, u32[]{:S(2)}) copy-start(bf16[8,128,512]{2,1,0:T(8,128)(2,1)} %param.15) | copy-start | bytes 3145732
  6.5 86.6 %all-gather.3.cloned.1.call-start = ((), (), s32[]{:S(2)}) async-start(), calls=%async_computation.1 | async-start | bytes 8912896 | tf_op jit(solution)/shard_map/all_gather | solution.py:15
  6.5 17.3 %copy-start.4 = (s32[16]{0:T(128)S(1)}, s32[16]{0:T(128)}, u32[]{:S(2)}) copy-start(s32[16]{0:T(128)} %param.10) | copy-start | bytes 196
  15.9 119.3 %all-gather.5.cloned.1.call-start = ((), (), s32[]{:S(2)}) async-start(), calls=%async_computation.2 | async-start | bytes 2228224 | tf_op jit(solution)/shard_map/all_gather | solution.py:16
  23.6 406.6 %reduce-scatter.2.cloned.1.call-start = ((), (), s32[]{:S(2)}) async-start(), calls=%async_computation.3 | async-start | bytes 17825792 | tf_op jit(solution)/shard_map/reduce_scatter | solution.py:30
  252.8 0.7 copy-start.5
  252.8 283.8 %copy-start.3 = (bf16[16,4,7168]{2,1,0:T(4,128)(2,1)S(1)}, bf16[16,4,7168]{2,1,0:T(4,128)(2,1)}, u32[]{:S(2)}) copy-start(bf16[16,4,7168]{2,1,0:T(4,128)(2,1)} %param.9) | copy-start | bytes 2752516
  252.9 283.7 %all-reduce.3.cloned.1.call-start = ((), (), s32[]{:S(2)}) async-start(), calls=%async_computation.4 | async-start | bytes 3670016 | tf_op jit(solution)/shard_map/psum | solution.py:35
  430.3 109.8 %copy-start.1 = (bf16[16,1024,64]{1,2,0:T(8,128)(2,1)S(1)}, bf16[16,1024,64]{1,2,0:T(8,128)(2,1)}, u32[]{:S(2)}) copy-start(bf16[16,1024,64]{1,2,0:T(8,128)(2,1)} %param.12) | copy-start | bytes 6291460
Sparse Core Ops, SparseCore 0:
  16.0 77.0 all-gather.2
  95.3 39.8 all-gather.4
  253.0 177.2 reduce-scatter.1
  440.4 96.1 all-reduce.2
where the time goes:
time: 548 us; the launch traced here: 547 us
  waiting for transfers between devices  286 us (52%)
  blocking collectives  116 us (21%)
  matrix products  109 us (20%)
  other arithmetic  17.7 us (3%)
  between operations  13.9 us (3%)
    reduce_scatter x1, waiting for transfers between devices, local_step(): lax.psum_scatter(o_part * rescale[..., None], 'seq', scatter_dimension=2,...  113 us
    psum x1, waiting for transfers between devices, local_step(): y_sum = lax.psum(y_part, 'seq')  96.4 us
    all_gather x1, waiting for transfers between devices, local_step(): lat_all = lax.all_gather(q_lat, 'seq', axis=2, tiled=True)  69 us
    unnamed x1, blocking collectives  62 us
    pmax x1, blocking collectives, local_step(): global_max = lax.pmax(local_max, 'seq')  54.4 us
    dot_general x1, matrix products, local_step(): jnp.einsum('bqhc,btc->bqht', lat_all, c_kv, preferred_element_type=jnp.fl...  34.4 us
    dot_general x1, matrix products, local_step(): jnp.einsum('bqht,btc->bqhc', weights.astype(jnp.bfloat16), c_kv, preferre...  25.7 us
    dot_general x1, matrix products, local_step(): jnp.einsum('bqhr,btr->bqht', rope_all, k_r, preferred_element_type=jnp.fl...  23.3 us
  transfers between devices with their start and end apart: 4, of which 4 were waited for; matrix products, arithmetic and copies ran while one was open for 8% of the time, Pallas kernels for 0%

commit v1 on v0

v1 whole, which is shorter than its diff:
```python
import functools
import math

import jax
import jax.numpy as jnp
from jax import lax
from jax.experimental import pallas as pl
from jax.experimental.pallas import tpu as pltpu
from jax.sharding import PartitionSpec as P

MASK_FILL = -1e30
NZ, NY, NC = 4, 2, 2
MESH = pl.DeviceIdType.MESH
f32, bf16 = jnp.float32, jnp.bfloat16


def place():
    s = lax.axis_index("seq")
    return s, s // (NY * NC), (s // NC) % NY, s % NC


def seq_of(z, y, c):
    return (z * NY + y) * NC + c


def remote(src, dst, send_sem, recv_sem, seq):
    return pltpu.make_async_remote_copy(
        src_ref=src, dst_ref=dst, send_sem=send_sem, recv_sem=recv_sem,
        device_id={"seq": seq}, device_id_type=MESH)


def meet(peers):
    barrier = pltpu.get_barrier_semaphore()
    for p in peers:
        pl.semaphore_signal(barrier, inc=1, device_id={"seq": p}, device_id_type=MESH)
    pl.semaphore_wait(barrier, len(peers))


def columns(rows):
    pad = jnp.zeros((128 - rows.shape[0], 128), f32)
    return jnp.concatenate([rows, pad], axis=0).T


def attend_kernel(scale, lens, q_hbm, c_hbm, k_hbm, out,
                  qbuf, ck, kr, o_full, ml0, ml1, ml2, rc_c, ml_c, rc_y, ml_y, rc_z, ml_z, wcol,
                  q_sem, c_sem, k_sem,
                  az_s, az_r, ay_s, ay_r, ac_s, ac_r,
                  oc_s, oc_r, oy_s, oy_r, oz_s, oz_r,
                  mc_s, mc_r, my_s, my_r, mz_s, mz_r):
    nb, slots = q_hbm.shape[0], ck.shape[0]
    local_len = ck.shape[1]
    s, z, y, c = place()
    core_peer, y_peer = seq_of(z, y, 1 - c), seq_of(z, 1 - y, c)
    zs = [lax.rem(z + d, NZ) for d in (1, 2, 3)]
    zf = [lax.rem(z + NZ - d, NZ) for d in (1, 2, 3)]
    base = c * 8 + y * 4
    mine = base + z

    own_q = pltpu.make_async_copy(q_hbm, qbuf.at[:, mine], q_sem)
    own_q.start()

    def cache(b):
        k = lax.rem(b, slots)
        return (pltpu.make_async_copy(c_hbm.at[b], ck.at[k], c_sem.at[k]),
                pltpu.make_async_copy(k_hbm.at[b], kr.at[k], k_sem.at[k]))

    for b in range(slots - 1):
        for cp in cache(b):
            cp.start()

    meet([core_peer, y_peer] + [seq_of(p, y, c) for p in zs])
    own_q.wait()

    def gather_z(b, d, peer, blk):
        return remote(qbuf.at[b, blk], qbuf.at[b, blk], az_s.at[b, d], az_r.at[b, d], seq_of(peer, y, c))

    def gather_y(b, yy):
        part = qbuf.at[b, pl.ds(c * 8 + yy * 4, 4)]
        return remote(part, part, ay_s.at[b], ay_r.at[b], y_peer)

    def gather_c(b, cc):
        part = qbuf.at[b, pl.ds(cc * 8, 8)]
        return remote(part, part, ac_s.at[b], ac_r.at[b], core_peer)

    def sum_c(b):
        return (remote(o_full.at[b, pl.ds((1 - c) * 8, 8)], rc_c.at[b], oc_s.at[b], oc_r.at[b], core_peer),
                remote(ml0.at[b, 1 - c], ml_c.at[b], mc_s.at[b], mc_r.at[b], core_peer))

    def sum_y(b):
        return (remote(o_full.at[b, pl.ds(c * 8 + (1 - y) * 4, 4)], rc_y.at[b], oy_s.at[b], oy_r.at[b], y_peer),
                remote(ml1.at[b], ml_y.at[b], my_s.at[b], my_r.at[b], y_peer))

    def sum_z(b, d):
        peer = seq_of(zs[d], y, c)
        return (remote(o_full.at[b, base + zs[d]], rc_z.at[d, b], oz_s.at[b, d], oz_r.at[b, d], peer),
                remote(ml2.at[b], ml_z.at[d, b], mz_s.at[b, d], mz_r.at[b, d], peer))

    def send_z(b):
        for d in range(3):
            gather_z(b, d, zs[d], mine).start()

    def step_a(b):
        for d in range(3):
            gather_z(b, d, zs[d], base + zf[d]).wait_recv()
        gather_y(b, y).start()

    def step_b(b):
        gather_y(b, 1 - y).wait_recv()
        gather_c(b, c).start()

    def attend(b):
        gather_c(b, 1 - c).wait_recv()
        for cp in cache(b):
            cp.wait()

        @pl.when(b + slots - 1 < nb)
        def _():
            for cp in cache(b + slots - 1):
                cp.start()

        k = lax.rem(b, slots)
        row_len = lens[b]
        pos = s * local_len + lax.broadcasted_iota(jnp.int32, (256, local_len), 1)
        token = lax.rem(lax.broadcasted_iota(jnp.int32, (256, 1), 0), 16) // 8
        lane = lax.broadcasted_iota(jnp.int32, (256, 128), 1)
        for hf in range(2):
            q = jnp.concatenate([qbuf[b, :, hf * 4 + j].reshape(256, 128) for j in range(4)], axis=1)
            qr = qbuf[b, :, 8].reshape(256, 128)[:, hf * 64:(hf + 1) * 64]
            sc = lax.dot_general(q, ck[k], (((1,), (1,)), ((), ())), preferred_element_type=f32)
            sc = sc + jnp.dot(qr, kr[k], preferred_element_type=f32)
            sc = jnp.where(pos <= row_len + hf * 2 + token, sc, MASK_FILL)
            m = jnp.max(sc, axis=1, keepdims=True)
            p = jnp.exp2((sc - m) * scale)
            l = jnp.sum(p, axis=1, keepdims=True)
            o = jnp.dot(p.astype(bf16), ck[k], preferred_element_type=f32)
            o_full[b, :, hf * 16:(hf + 1) * 16, :] = o.reshape(16, 16, o.shape[1])
            stat = jnp.where(lane == 0, m * scale, jnp.where(lane == 1, l, 0.0)).T
            for cc in range(2):
                ml0[b, cc, hf * 2:hf * 2 + 2, :] = stat[0:2, cc * 128:(cc + 1) * 128]
        for cp in sum_c(b):
            cp.start()

    def merge_stats(a, r):
        stats, factors = [], []
        for hf in range(2):
            ma, la, mb, lb = (a[2 * hf:2 * hf + 1], a[2 * hf + 1:2 * hf + 2], r[2 * hf:2 * hf + 1], r[2 * hf + 1:2 * hf + 2])
            top = jnp.maximum(ma, mb)
            wa, wb = jnp.exp2(ma - top), jnp.exp2(mb - top)
            stats += [top, la * wa + lb * wb]
            factors += [wa, wb]
        return jnp.concatenate(stats, axis=0), columns(jnp.concatenate(factors, axis=0))

    def step_d(b):
        for cp in sum_c(b):
            cp.wait_recv()
        stats, cols = merge_stats(ml0[b, c, 0:4], ml_c[b, 0:4])
        ml1[b, 0:4, :] = stats
        for hf in range(2):
            rows = pl.ds(hf * 16, 16)
            wa, wb = (cols[:, 2 * hf + j:2 * hf + j + 1].reshape(8, 16, 1) for j in range(2))
            part = pl.ds(c * 8, 8)
            o_full[b, part, rows, :] = o_full[b, part, rows, :] * wa + rc_c[b, :, rows, :] * wb
        for cp in sum_y(b):
            cp.start()

    def step_e(b):
        for cp in sum_y(b):
            cp.wait_recv()
        stats, cols = merge_stats(ml1[b, 0:4], ml_y[b, 0:4])
        ml2[b, 0:4, :] = stats
        wcol[...] = cols
        cols = wcol[pl.ds(pl.multiple_of(y * 64, 64), 64), :]
        for hf in range(2):
            rows = pl.ds(hf * 16, 16)
            wa, wb = (cols[:, 2 * hf + j:2 * hf + j + 1].reshape(4, 16, 1) for j in range(2))
            part = pl.ds(base, 4)
            o_full[b, part, rows, :] = o_full[b, part, rows, :] * wa + rc_y[b, :, rows, :] * wb
        for d in range(3):
            for cp in sum_z(b, d):
                cp.start()

    def step_f(b):
        for d in range(3):
            for cp in sum_z(b, d):
                cp.wait_recv()
        parts = [ml2[b, 0:4]] + [ml_z[d, b, 0:4] for d in range(3)]
        factors = []
        for hf in range(2):
            ms, ls = [p[2 * hf:2 * hf + 1] for p in parts], [p[2 * hf + 1:2 * hf + 2] for p in parts]
            top = functools.reduce(jnp.maximum, ms)
            ws = [jnp.exp2(m - top) for m in ms]
            total = sum(w * l for w, l in zip(ws, ls))
            factors += [w / total for w in ws]
        wcol[...] = columns(jnp.concatenate(factors, axis=0))
        cols = wcol[pl.ds(pl.multiple_of((y * 4 + z) * 16, 16), 16), :]
        for hf in range(2):
            rows = pl.ds(hf * 16, 16)
            w = [cols[:, 4 * hf + j:4 * hf + j + 1] for j in range(4)]
            o = o_full[b, mine, rows, :] * w[0]
            for d in range(3):
                o = o + rc_z[d, b, rows, :] * w[d + 1]
            out[b, rows, :] = o.astype(bf16)

    ahead = 3
    for b in range(ahead):
        send_z(b)

    steps = ((0, -ahead, send_z), (0, 0, step_a), (0, 1, step_b), (0, 4, step_d), (0, 6, step_e), (0, 8, step_f), (0, 2, attend))

    @pl.loop(0, nb + 8)
    def _(it):
        for _, lag, fn in steps:
            b = it - lag

            @pl.when((b >= 0) & (b < nb))
            def _(fn=fn, b=b):
                fn(b)

    @pl.loop(0, nb)
    def _(b):
        gather_y(b, y).wait_send()
        gather_c(b, c).wait_send()
        for d in range(3):
            gather_z(b, d, zs[d], mine).wait_send()
            for cp in sum_z(b, d):
                cp.wait_send()
        for cp in sum_c(b) + sum_y(b):
            cp.wait_send()


def attend_all(q, lens, c_kv, k_t, score_scale):
    nb, local_len, lat = c_kv.shape
    slots = 3
    dma = pltpu.SemaphoreType.DMA
    return pl.pallas_call(
        functools.partial(attend_kernel, score_scale * math.log2(math.e)),
        out_shape=jax.ShapeDtypeStruct((nb, 32, lat), bf16),
        in_specs=[pl.BlockSpec(memory_space=pltpu.SMEM)] + [pl.BlockSpec(memory_space=pl.ANY)] * 3,
        out_specs=pl.BlockSpec(memory_space=pltpu.VMEM),
        scratch_shapes=[
            pltpu.VMEM((nb, 16, 9, 16, 128), bf16),
            pltpu.VMEM((slots, local_len, lat), bf16),
            pltpu.VMEM((slots, k_t.shape[1], local_len), bf16),
            pltpu.VMEM((nb, 16, 32, lat), f32),
            pltpu.VMEM((nb, 2, 8, 128), f32),
            pltpu.VMEM((nb, 8, 128), f32),
            pltpu.VMEM((nb, 8, 128), f32),
            pltpu.VMEM((nb, 8, 32, lat), f32),
            pltpu.VMEM((nb, 8, 128), f32),
            pltpu.VMEM((nb, 4, 32, lat), f32),
            pltpu.VMEM((nb, 8, 128), f32),
            pltpu.VMEM((3, nb, 32, lat), f32),
            pltpu.VMEM((3, nb, 8, 128), f32),
            pltpu.VMEM((128, 128), f32),
            dma, dma((slots,)), dma((slots,)),
            dma((nb, 3)), dma((nb, 3)), dma((nb,)), dma((nb,)), dma((nb,)), dma((nb,)),
            dma((nb,)), dma((nb,)), dma((nb,)), dma((nb,)), dma((nb, 3)), dma((nb, 3)),
            dma((nb,)), dma((nb,)), dma((nb,)), dma((nb,)), dma((nb, 3)), dma((nb, 3)),
        ],
        compiler_params=pltpu.CompilerParams(
            collective_id=0, has_side_effects=True, vmem_limit_bytes=64 * 1024 * 1024 - 65536),
        name="attend_all",
    )(lens, q, c_kv, k_t)


def total_kernel(y_ref, h_ref, out, acc, rc1, rc2, gat, s1, r1, s2, r2, s3, r3, s4, r4):
    _, z, y, c = place()
    rows, half = y_ref.shape[0], y_ref.shape[1] // 2
    wide, deep = half // NY, rows // NZ
    core_peer = seq_of(z, y, 1 - c)
    me = z * NY + y
    tos = [lax.rem(me + d, 8) for d in range(1, 8)]
    froms = [lax.rem(me + 8 - d, 8) for d in range(1, 8)]
    meet([core_peer] + [t * NC + c for t in tos])

    def lanes(cc):
        return pl.ds(pl.multiple_of(cc * half, 128), half)

    swap = remote(y_ref.at[:, lanes(1 - c)], rc1, s1, r1, core_peer)
    swap.start()
    swap.wait_recv()
    acc[...] = y_ref[:, lanes(c)] + rc1[...]

    def piece(chip):
        return pl.ds((chip // NY) * deep, deep), pl.ds(pl.multiple_of((chip % NY) * wide, 128), wide)

    def out_piece(chip):
        return pl.ds((chip // NY) * deep, deep), pl.ds(pl.multiple_of(c * half + (chip % NY) * wide, 128), wide)

    first = [remote(acc.at[piece(tos[d])], rc2.at[d], s2.at[d], r2.at[d], tos[d] * NC + c) for d in range(7)]
    for cp in first:
        cp.start()
    for cp in first:
        cp.wait_recv()
    total = acc[piece(me)]
    for d in range(7):
        total = total + rc2[d]
    gat[out_piece(me)] = (h_ref[out_piece(me)].astype(f32) + total).astype(bf16)
    second = [remote(gat.at[out_piece(me)], gat.at[out_piece(me)], s3.at[d], r3.at[d], tos[d] * NC + c) for d in range(7)]
    for cp in second:
        cp.start()
    for d in range(7):
        blk = gat.at[out_piece(froms[d])]
        remote(blk, blk, s3.at[d], r3.at[d], tos[d] * NC + c).wait_recv()
    last = remote(gat.at[:, lanes(c)], gat.at[:, lanes(c)], s4, r4, core_peer)
    last.start()
    other = gat.at[:, lanes(1 - c)]
    remote(other, other, s4, r4, core_peer).wait_recv()
    out[...] = gat[...]
    for cp in [swap, last] + first + second:
        cp.wait_send()


def total_all(y_part, hidden):
    n, dim = y_part.shape
    dma = pltpu.SemaphoreType.DMA
    vm = pl.BlockSpec(memory_space=pltpu.VMEM)
    return pl.pallas_call(
        total_kernel,
        out_shape=jax.ShapeDtypeStruct((n, dim), bf16),
        in_specs=[vm, vm],
        out_specs=vm,
        scratch_shapes=[
            pltpu.VMEM((n, dim // 2), f32), pltpu.VMEM((n, dim // 2), f32),
            pltpu.VMEM((7, n // NZ, dim // 4), f32), pltpu.VMEM((n, dim), bf16),
            dma, dma, dma((7,)), dma((7,)), dma((7,)), dma((7,)), dma, dma,
        ],
        compiler_params=pltpu.CompilerParams(
            collective_id=1, has_side_effects=True, vmem_limit_bytes=32 * 1024 * 1024),
        name="total_all",
    )(y_part, hidden)


def solution(mesh):
    def local_step(hidden, cache_lens, c_kv, k_r, w_uq, w_qr, w_uk, w_uv, w_o):
        score_scale = (w_uq.shape[2] + w_qr.shape[2]) ** -0.5
        nb, nq, dim = hidden.shape
        nh, lat = w_uk.shape[0], w_uk.shape[2]
        q_nope = jnp.einsum("cre,eil->cril", hidden, w_uq, preferred_element_type=f32).astype(bf16)
        q_rope = jnp.einsum("cre,eis->cris", hidden, w_qr, preferred_element_type=f32).astype(bf16)
        q_lat = jnp.einsum("bqhk,hkc->bqhc", q_nope, w_uk, preferred_element_type=f32).astype(bf16)
        q_a = q_lat.reshape(nb, 2, 16, 4, 128).transpose(0, 1, 3, 2, 4).reshape(nb, 8, 16, 128)
        q_b = q_rope.reshape(nb, 2, 16, 64).transpose(0, 2, 1, 3).reshape(nb, 1, 16, 128)
        q = jnp.concatenate([q_a, q_b], axis=1)
        o_lat = attend_all(q, cache_lens, c_kv, jnp.swapaxes(k_r, 1, 2), score_scale)
        o_lat = o_lat.reshape(nb * nq, nh, lat)
        o_val = jnp.einsum("nhc,hcv->nhv", o_lat, w_uv, preferred_element_type=f32).astype(bf16)
        y_part = jnp.einsum("niw,iwe->ne", o_val, w_o, preferred_element_type=f32)
        return total_all(y_part, hidden.reshape(nb * nq, dim)).reshape(nb, nq, dim)

    specs_in = (P("batch", None, None), P("batch"), P("batch", "seq", None), P("batch", "seq", None),
                P(None, "seq", None), P(None, "seq", None), P("seq", None, None), P("seq", None, None),
                P("seq", None, None))
    return jax.shard_map(local_step, mesh=mesh, in_specs=specs_in, out_specs=P("batch", None, None), check_vma=False)
```

time: 548 us -> 247 us (0.45)
  waiting for transfers between devices: 286 us -> 0 us
  Pallas kernels: 0 us -> 215 us
  blocking collectives: 116 us -> 0 us
  matrix products: 109 us -> 22.8 us
  other arithmetic: 17.7 us -> 0.87 us
  between operations: 13.9 us -> 0.09 us
    pallas_call x0 -> x2, Pallas kernels: none -> 215 us  [the longest x1 173 us: attend_all(): pl.pallas_call(functools.partial(attend_kernel, score_scale * math.log2(m...]
    reduce_scatter x1 -> x0, waiting for transfers between devices: 113 us -> none  [local_step(): lax.psum_scatter(o_part * rescale[..., None], 'seq', scatter_dimension=2,...]
    psum x1 -> x0, waiting for transfers between devices: 96.4 us -> none  [local_step(): y_sum = lax.psum(y_part, 'seq')]
    dot_general x7 -> x3, matrix products: 109 us -> 22.8 us  [the longest x1 8.5 us: local_step(): jnp.einsum('bqhk,hkc->bqhc', q_nope, w_uk, preferred_element_type=f32)]
    all_gather x2 -> x0, waiting for transfers between devices: 76.7 us -> none  [the longest x1 69 us: local_step(): lat_all = lax.all_gather(q_lat, 'seq', axis=2, tiled=True)]
    unnamed x1 -> x0, blocking collectives: 62 us -> none
    pmax x1 -> x0, blocking collectives: 54.4 us -> none  [local_step(): global_max = lax.pmax(local_max, 'seq')]
    reduce_sum x1 -> x0, other arithmetic: 14.2 us -> none  [local_step(): local_sum = jnp.sum(weights, axis=-1)]
  transfers between devices with their start and end apart: 4 -> 0, of which waited for: 4 -> 0; matrix products, arithmetic and copies ran while one was open for 8% -> 0% of each run, Pallas kernels for 0% -> 0%
where the time goes in v1:
time: 247 us; the launch traced here: 244 us
  Pallas kernels  215 us (87%)
  matrix products  22.8 us (9%)
  local copies, waits for them, and re-layouts  5.87 us (2%)
    pallas_call x1, Pallas kernels, attend_all(): pl.pallas_call(functools.partial(attend_kernel, score_scale * math.log2(m...  173 us
    pallas_call x1, Pallas kernels, total_all(): pl.pallas_call(total_kernel, out_shape=jax.ShapeDtypeStruct((n, dim), bf1...  41.2 us
    dot_general x1, matrix products, local_step(): jnp.einsum('bqhk,hkc->bqhc', q_nope, w_uk, preferred_element_type=f32)  8.5 us
    dot_general x1, matrix products, local_step(): y_part = jnp.einsum('niw,iwe->ne', o_val, w_o, preferred_element_type=f32)  7.3 us
    dot_general x1, matrix products, local_step(): jnp.einsum('cre,eis->cris', hidden, w_qr, preferred_element_type=f32)  6.99 us

profile of v1, /device:TPU:1, one launch (start us, length us, event | category | flops | bytes accessed | tf_op | source)
XLA Modules:
  0.0 244.3 jit_solution(3946064166367354163)
XLA Ops:
  0.0 7.0 %fusion.5 = bf16[16,4,8,64]{3,0,2,1:T(8,128)(2,1)S(1)} fusion(bf16[7168,8,64]{0,2,1:T(8,128)(2,1)} %param.14, bf16[16,4,7168,1]{2,1,0,3:T(4,128)(2,1)} %bitcast.37), kind=kOutput, calls=%fused_computation.7 | convolution fusion | flops 469794816 | bytes 8323072 | tf_op jit(solution)/shard_map/cre,eis->cris/dot_general | solution.py:340
  7.0 0.1 copy.39
  7.1 0.1 reshape.24
  7.3 8.5 %fusion.4 = bf16[16,4,8,512]{3,0,1,2:T(8,128)(2,1)S(1)} fusion(bf16[8,128,512]{2,1,0:T(8,128)(2,1)} %param.15, bf16[7168,8,128,1]{2,1,0,3:T(8,128)(2,1)} %bitcast.41, bf16[16,4,7168,1]{2,1,0,3:T(4,128)(2,1)} %bitcast.38), kind=kOutput, calls=%fused_computation.6 | convolution fusion | flops 1006960640 | bytes 17170432 | tf_op jit(solution)/shard_map/bqhk,hkc->bqhc/dot_general | solution.py:341
  15.8 0.3 copy.12
  16.1 0.1 reshape.21
  16.2 0.1 copy.13
  16.3 0.9 pad_maximum_fusion.q_hbm
  17.2 173.4 %attend_all.1 = bf16[16,32,512]{2,1,0:T(8,128)(2,1)} custom-call(s32[16]{0:T(128)} %lens.1, bf16[16,9,16,128]{3,2,1,0:T(8,128)(2,1)} %pad_maximum_fusion.q_hbm, bf16[16,1024,512]{2,1,0:T(8,128)(2,1)} %c_hbm.1, bf16[16,64,1024]{2,1,0:T(8,128)(2,1)} %bitcast.33), custom_call_target="tpu_custom_call" | custom-call | tf_op jit(solution)/shard_map/attend_all/pallas_call | solution.py:235
  190.6 1.7 reshape.26.h_ref
  192.3 7.3 %convolution_bitcast_fusion.y_ref = f32[64,7168]{1,0:T(8,128)S(1)} fusion(bf16[8,128,7168]{2,1,0:T(8,128)(2,1)} %param.17, bf16[8,512,128]{2,1,0:T(8,128)(2,1)} %param.16, bf16[64,8,512]{2,1,0:T(8,128)(2,1)} %bitcast.34), kind=kOutput, calls=%fused_computation.2 | convolution fusion | flops 1006698496 | bytes 18087936 | tf_op jit(solution)/shard_map/niw,iwe->ne/dot_general | solution.py:348
  199.6 41.2 %total_all.1 = bf16[64,7168]{1,0:T(8,128)(2,1)S(1)} custom-call(f32[64,7168]{1,0:T(8,128)S(1)} %convolution_bitcast_fusion.y_ref, bf16[64,7168]{1,0:T(8,128)(2,1)S(1)} %reshape.26.h_ref), custom_call_target="tpu_custom_call" | custom-call | tf_op jit(solution)/shard_map/total_all/pallas_call | solution.py:318
  240.8 0.0 copy-start
  240.8 0.9 copy-done
  241.8 2.5 %reshape.27 = bf16[16,4,7168]{2,1,0:T(4,128)(2,1)} reshape(bf16[64,7168]{1,0:T(8,128)(2,1)} %copy-done) | data formatting | bytes 1835008 | tf_op jit(solution)/shard_map/reshape | solution.py:349
Async XLA Ops:
  240.8 0.9 copy-start

commit v2 on v1

--- a/solution.py
+++ b/solution.py
@@ -42,21 +42,19 @@
 
 
 def attend_kernel(scale, lens, q_hbm, c_hbm, k_hbm, out,
-                  qbuf, ck, kr, o_full, ml0, ml1, ml2, rc_c, ml_c, rc_y, ml_y, rc_z, ml_z, wcol,
+                  qbuf, ck, kr, o_full, ml0, ml1, ml2, rc_c, ml_c, rc_y, ml_y,
+                  rc_u, ml_u, ml_us, rc_d, ml_d, ml_ds, wcol,
                   q_sem, c_sem, k_sem,
-                  az_s, az_r, ay_s, ay_r, ac_s, ac_r,
-                  oc_s, oc_r, oy_s, oy_r, oz_s, oz_r,
-                  mc_s, mc_r, my_s, my_r, mz_s, mz_r):
+                  ay_s, ay_r, au_s, au_r, ad_s, ad_r, ac_s, ac_r,
+                  oc_s, oc_r, oy_s, oy_r, ou_s, ou_r, od_s, od_r,
+                  mc_s, mc_r, my_s, my_r, mu_s, mu_r, md_s, md_r):
     nb, slots = q_hbm.shape[0], ck.shape[0]
     local_len = ck.shape[1]
     s, z, y, c = place()
     core_peer, y_peer = seq_of(z, y, 1 - c), seq_of(z, 1 - y, c)
-    zs = [lax.rem(z + d, NZ) for d in (1, 2, 3)]
-    zf = [lax.rem(z + NZ - d, NZ) for d in (1, 2, 3)]
-    base = c * 8 + y * 4
-    mine = base + z
-
-    own_q = pltpu.make_async_copy(q_hbm, qbuf.at[:, mine], q_sem)
+    upper, lower = seq_of(lax.rem(z + 1, NZ), y, c), seq_of(lax.rem(z + NZ - 1, NZ), y, c)
+
+    own_q = pltpu.make_async_copy(q_hbm, qbuf.at[:, c, y, z], q_sem)
     own_q.start()
 
     def cache(b):
@@ -68,44 +66,80 @@
         for cp in cache(b):
             cp.start()
 
-    meet([core_peer, y_peer] + [seq_of(p, y, c) for p in zs])
+    meet([core_peer, y_peer, upper, lower])
     own_q.wait()
 
-    def gather_z(b, d, peer, blk):
-        return remote(qbuf.at[b, blk], qbuf.at[b, blk], az_s.at[b, d], az_r.at[b, d], seq_of(peer, y, c))
-
     def gather_y(b, yy):
-        part = qbuf.at[b, pl.ds(c * 8 + yy * 4, 4)]
+        part = qbuf.at[b, c, yy, z]
         return remote(part, part, ay_s.at[b], ay_r.at[b], y_peer)
 
+    def gather_up(b, origin, d):
+        part = qbuf.at[b, c, :, origin]
+        return remote(part, part, au_s.at[b, d - 1], au_r.at[b, d - 1], upper)
+
+    def gather_down(b, origin, d):
+        part = qbuf.at[b, c, :, origin]
+        return remote(part, part, ad_s.at[b, d - 1], ad_r.at[b, d - 1], lower)
+
     def gather_c(b, cc):
-        part = qbuf.at[b, pl.ds(cc * 8, 8)]
+        part = qbuf.at[b, cc]
         return remote(part, part, ac_s.at[b], ac_r.at[b], core_peer)
 
-    def sum_c(b):
-        return (remote(o_full.at[b, pl.ds((1 - c) * 8, 8)], rc_c.at[b], oc_s.at[b], oc_r.at[b], core_peer),
-                remote(ml0.at[b, 1 - c], ml_c.at[b], mc_s.at[b], mc_r.at[b], core_peer))
+    def sum_c(b, hf):
+        rows = pl.ds(hf * 16, 16)
+        return remote(o_full.at[b, 1 - c, :, :, rows], rc_c.at[b, :, :, rows], oc_s.at[b, hf], oc_r.at[b, hf], core_peer)
+
+    def stat_c(b):
+        return remote(ml0.at[b, 1 - c], ml_c.at[b], mc_s.at[b], mc_r.at[b], core_peer)
 
     def sum_y(b):
-        return (remote(o_full.at[b, pl.ds(c * 8 + (1 - y) * 4, 4)], rc_y.at[b], oy_s.at[b], oy_r.at[b], y_peer),
+        return (remote(o_full.at[b, c, 1 - y], rc_y.at[b], oy_s.at[b], oy_r.at[b], y_peer),
                 remote(ml1.at[b], ml_y.at[b], my_s.at[b], my_r.at[b], y_peer))
 
-    def sum_z(b, d):
-        peer = seq_of(zs[d], y, c)
-        return (remote(o_full.at[b, base + zs[d]], rc_z.at[d, b], oz_s.at[b, d], oz_r.at[b, d], peer),
-                remote(ml2.at[b], ml_z.at[d, b], mz_s.at[b, d], mz_r.at[b, d], peer))
-
-    def send_z(b):
-        for d in range(3):
-            gather_z(b, d, zs[d], mine).start()
-
-    def step_a(b):
-        for d in range(3):
-            gather_z(b, d, zs[d], base + zf[d]).wait_recv()
-        gather_y(b, y).start()
-
-    def step_b(b):
+    def sum_up(b, dest, d):
+        return remote(o_full.at[b, c, y, dest], rc_u.at[b, dest], ou_s.at[b, d - 1], ou_r.at[b, d - 1], upper)
+
+    def stat_up(b, stat):
+        return remote(stat.at[b], ml_u.at[b], mu_s.at[b], mu_r.at[b], upper)
+
+    def sum_down(b, dest, d):
+        return remote(o_full.at[b, c, y, dest], rc_d.at[b, dest], od_s.at[b, d - 1], od_r.at[b, d - 1], lower)
+
+    def stat_down(b, stat):
+        return remote(stat.at[b], ml_d.at[b], md_s.at[b], md_r.at[b], lower)
+
+    def pass_on(b, d):
+        @pl.when((z < NZ - 1) & (z - (d - 1) >= 0))
+        def _():
+            gather_up(b, z - (d - 1), d).start()
+
+        @pl.when((z > 0) & (z + (d - 1) < NZ))
+        def _():
+            gather_down(b, z + (d - 1), d).start()
+
+    def arrive(b, d):
+        @pl.when(z - d >= 0)
+        def _():
+            gather_up(b, z - d, d).wait_recv()
+
+        @pl.when(z + d < NZ)
+        def _():
+            gather_down(b, z + d, d).wait_recv()
+
+    def step_z1(b):
         gather_y(b, 1 - y).wait_recv()
+        pass_on(b, 1)
+
+    def step_z2(b):
+        arrive(b, 1)
+        pass_on(b, 2)
+
+    def step_z3(b):
+        arrive(b, 2)
+        pass_on(b, 3)
+
+    def step_z4(b):
+        arrive(b, 3)
         gather_c(b, c).start()
 
     def attend(b):
@@ -124,8 +158,8 @@
         token = lax.rem(lax.broadcasted_iota(jnp.int32, (256, 1), 0), 16) // 8
         lane = lax.broadcasted_iota(jnp.int32, (256, 128), 1)
         for hf in range(2):
-            q = jnp.concatenate([qbuf[b, :, hf * 4 + j].reshape(256, 128) for j in range(4)], axis=1)
-            qr = qbuf[b, :, 8].reshape(256, 128)[:, hf * 64:(hf + 1) * 64]
+            q = jnp.concatenate([qbuf[b, :, :, :, hf * 4 + j].reshape(256, 128) for j in range(4)], axis=1)
+            qr = qbuf[b, :, :, :, 8].reshape(256, 128)[:, hf * 64:(hf + 1) * 64]
             sc = lax.dot_general(q, ck[k], (((1,), (1,)), ((), ())), preferred_element_type=f32)
             sc = sc + jnp.dot(qr, kr[k], preferred_element_type=f32)
             sc = jnp.where(pos <= row_len + hf * 2 + token, sc, MASK_FILL)
@@ -133,83 +167,141 @@
             p = jnp.exp2((sc - m) * scale)
             l = jnp.sum(p, axis=1, keepdims=True)
             o = jnp.dot(p.astype(bf16), ck[k], preferred_element_type=f32)
-            o_full[b, :, hf * 16:(hf + 1) * 16, :] = o.reshape(16, 16, o.shape[1])
+            o_full[b, :, :, :, hf * 16:(hf + 1) * 16, :] = o.reshape(2, 2, 4, 16, o.shape[1])
             stat = jnp.where(lane == 0, m * scale, jnp.where(lane == 1, l, 0.0)).T
             for cc in range(2):
                 ml0[b, cc, hf * 2:hf * 2 + 2, :] = stat[0:2, cc * 128:(cc + 1) * 128]
-        for cp in sum_c(b):
-            cp.start()
-
-    def merge_stats(a, r):
+            sum_c(b, hf).start()
+        stat_c(b).start()
+
+    def merge_stats(parts, final):
         stats, factors = [], []
-        for hf in range(2):
-            ma, la, mb, lb = (a[2 * hf:2 * hf + 1], a[2 * hf + 1:2 * hf + 2], r[2 * hf:2 * hf + 1], r[2 * hf + 1:2 * hf + 2])
-            top = jnp.maximum(ma, mb)
-            wa, wb = jnp.exp2(ma - top), jnp.exp2(mb - top)
-            stats += [top, la * wa + lb * wb]
-            factors += [wa, wb]
-        return jnp.concatenate(stats, axis=0), columns(jnp.concatenate(factors, axis=0))
-
-    def step_d(b):
-        for cp in sum_c(b):
-            cp.wait_recv()
-        stats, cols = merge_stats(ml0[b, c, 0:4], ml_c[b, 0:4])
-        ml1[b, 0:4, :] = stats
-        for hf in range(2):
-            rows = pl.ds(hf * 16, 16)
-            wa, wb = (cols[:, 2 * hf + j:2 * hf + j + 1].reshape(8, 16, 1) for j in range(2))
-            part = pl.ds(c * 8, 8)
-            o_full[b, part, rows, :] = o_full[b, part, rows, :] * wa + rc_c[b, :, rows, :] * wb
-        for cp in sum_y(b):
-            cp.start()
-
-    def step_e(b):
-        for cp in sum_y(b):
-            cp.wait_recv()
-        stats, cols = merge_stats(ml1[b, 0:4], ml_y[b, 0:4])
-        ml2[b, 0:4, :] = stats
-        wcol[...] = cols
-        cols = wcol[pl.ds(pl.multiple_of(y * 64, 64), 64), :]
-        for hf in range(2):
-            rows = pl.ds(hf * 16, 16)
-            wa, wb = (cols[:, 2 * hf + j:2 * hf + j + 1].reshape(4, 16, 1) for j in range(2))
-            part = pl.ds(base, 4)
-            o_full[b, part, rows, :] = o_full[b, part, rows, :] * wa + rc_y[b, :, rows, :] * wb
-        for d in range(3):
-            for cp in sum_z(b, d):
-                cp.start()
-
-    def step_f(b):
-        for d in range(3):
-            for cp in sum_z(b, d):
-                cp.wait_recv()
-        parts = [ml2[b, 0:4]] + [ml_z[d, b, 0:4] for d in range(3)]
-        factors = []
         for hf in range(2):
             ms, ls = [p[2 * hf:2 * hf + 1] for p in parts], [p[2 * hf + 1:2 * hf + 2] for p in parts]
             top = functools.reduce(jnp.maximum, ms)
             ws = [jnp.exp2(m - top) for m in ms]
             total = sum(w * l for w, l in zip(ws, ls))
-            factors += [w / total for w in ws]
-        wcol[...] = columns(jnp.concatenate(factors, axis=0))
-        cols = wcol[pl.ds(pl.multiple_of((y * 4 + z) * 16, 16), 16), :]
+            stats += [top, total]
+            factors += [w / total for w in ws] if final else ws
+        return jnp.concatenate(stats, axis=0), columns(jnp.concatenate(factors, axis=0))
+
+    def step_d(b):
+        for hf in range(2):
+            sum_c(b, hf).wait_recv()
+        stat_c(b).wait_recv()
+        stats, cols = merge_stats([ml0[b, c, 0:4], ml_c[b, 0:4]], False)
+        ml1[b, 0:4, :] = stats
         for hf in range(2):
             rows = pl.ds(hf * 16, 16)
-            w = [cols[:, 4 * hf + j:4 * hf + j + 1] for j in range(4)]
-            o = o_full[b, mine, rows, :] * w[0]
-            for d in range(3):
-                o = o + rc_z[d, b, rows, :] * w[d + 1]
+            wa, wb = (cols[:, 2 * hf + j:2 * hf + j + 1].reshape(2, 4, 16, 1) for j in range(2))
+            o_full[b, c, :, :, rows, :] = o_full[b, c, :, :, rows, :] * wa + rc_c[b, :, :, rows, :] * wb
+        for cp in sum_y(b):
+            cp.start()
+
+    def step_e(b):
+        for cp in sum_y(b):
+            cp.wait_recv()
+        stats, cols = merge_stats([ml1[b, 0:4], ml_y[b, 0:4]], False)
+        ml2[b, 0:4, :] = stats
+        wcol[...] = cols
+        cols = wcol[pl.ds(pl.multiple_of(y * 64, 64), 64), :]
+        for hf in range(2):
+            rows = pl.ds(hf * 16, 16)
+            wa, wb = (cols[:, 2 * hf + j:2 * hf + j + 1].reshape(4, 16, 1) for j in range(2))
+            o_full[b, c, y, :, rows, :] = o_full[b, c, y, :, rows, :] * wa + rc_y[b, :, rows, :] * wb
+
+        @pl.when(z == 0)
+        def _():
+            send_up(b, 0, ml2)
+
+        @pl.when(z == NZ - 1)
+        def _():
+            send_down(b, NZ - 1, ml2)
+
+    def send_up(b, at, stat):
+        for dest in range(at + 1, NZ):
+            sum_up(b, dest, dest - at).start()
+        stat_up(b, stat).start()
+
+    def send_down(b, at, stat):
+        for dest in range(at - 1, -1, -1):
+            sum_down(b, dest, at - dest).start()
+        stat_down(b, stat).start()
+
+    def recv_up(b, at, dests):
+        for dest in dests:
+            sum_up(b, dest, dest - at + 1).wait_recv()
+
+    def recv_down(b, at, dests):
+        for dest in dests:
+            sum_down(b, dest, at - dest + 1).wait_recv()
+
+    def relay(b, arrived, stat_in, stat_out, dests):
+        stats, cols = merge_stats([ml2[b, 0:4], stat_in[b, 0:4]], False)
+        stat_out[b, 0:4, :] = stats
+        wcol[...] = cols
+        for dest in dests:
+            cols = wcol[pl.ds(pl.multiple_of(y * 64 + dest * 16, 16), 16), :]
+            for hf in range(2):
+                rows = pl.ds(hf * 16, 16)
+                wa, wb = (cols[:, 2 * hf + j:2 * hf + j + 1] for j in range(2))
+                o_full[b, c, y, dest, rows, :] = o_full[b, c, y, dest, rows, :] * wa + arrived[b, dest, rows, :] * wb
+
+    def step_g(hop, b):
+        @pl.when(z == hop)
+        def _():
+            stat_up(b, ml2).wait_recv()
+            recv_up(b, hop, range(hop + 1, NZ))
+            relay(b, rc_u, ml_u, ml_us, range(hop + 1, NZ))
+            send_up(b, hop, ml_us)
+
+        at = NZ - 1 - hop
+
+        @pl.when(z == at)
+        def _():
+            stat_down(b, ml2).wait_recv()
+            recv_down(b, at, range(at - 1, -1, -1))
+            relay(b, rc_d, ml_d, ml_ds, range(at - 1, -1, -1))
+            send_down(b, at, ml_ds)
+
+    def finish(b, at):
+        parts, sums = [ml2[b, 0:4]], [o_full.at[b, c, y, at]]
+        if at > 0:
+            recv_up(b, at, [at])
+            if at == NZ - 1:
+                stat_up(b, ml2).wait_recv()
+            parts.append(ml_u[b, 0:4])
+            sums.append(rc_u.at[b, at])
+        if at < NZ - 1:
+            recv_down(b, at, [at])
+            if at == 0:
+                stat_down(b, ml2).wait_recv()
+            parts.append(ml_d[b, 0:4])
+            sums.append(rc_d.at[b, at])
+        wcol[...] = merge_stats(parts, True)[1]
+        cols = wcol[pl.ds(pl.multiple_of(y * 64 + at * 16, 16), 16), :]
+        n = len(parts)
+        for hf in range(2):
+            rows = pl.ds(hf * 16, 16)
+            o = sum(part[rows, :] * cols[:, n * hf + j:n * hf + j + 1] for j, part in enumerate(sums))
             out[b, rows, :] = o.astype(bf16)
 
-    ahead = 3
-    for b in range(ahead):
-        send_z(b)
-
-    steps = ((0, -ahead, send_z), (0, 0, step_a), (0, 1, step_b), (0, 4, step_d), (0, 6, step_e), (0, 8, step_f), (0, 2, attend))
-
-    @pl.loop(0, nb + 8)
+    def step_f(b):
+        for at in range(NZ):
+            @pl.when(z == at)
+            def _(at=at):
+                finish(b, at)
+
+    @pl.loop(0, nb)
+    def _(b):
+        gather_y(b, y).start()
+
+    steps = ((7, step_e), (8, functools.partial(step_g, 1)), (9, functools.partial(step_g, 2)), (10, step_f),
+             (0, step_z1), (1, step_z2), (2, step_z3), (3, step_z4), (5, step_d), (4, attend))
+
+    @pl.loop(0, nb + 10)
     def _(it):
-        for _, lag, fn in steps:
+        for lag, fn in steps:
             b = it - lag
 
             @pl.when((b >= 0) & (b < nb))
@@ -220,12 +312,30 @@
     def _(b):
         gather_y(b, y).wait_send()
         gather_c(b, c).wait_send()
-        for d in range(3):
-            gather_z(b, d, zs[d], mine).wait_send()
-            for cp in sum_z(b, d):
-                cp.wait_send()
-        for cp in sum_c(b) + sum_y(b):
+        for d in (1, 2, 3):
+            @pl.when((z < NZ - 1) & (z - (d - 1) >= 0))
+            def _(d=d):
+                gather_up(b, z - (d - 1), d).wait_send()
+
+            @pl.when((z > 0) & (z + (d - 1) < NZ))
+            def _(d=d):
+                gather_down(b, z + (d - 1), d).wait_send()
+        sum_c(b, 0).wait_send()
+        sum_c(b, 1).wait_send()
+        stat_c(b).wait_send()
+        for cp in sum_y(b):
             cp.wait_send()
+        for at in range(NZ):
+            @pl.when(z == at)
+            def _(at=at):
+                for dest in range(at + 1, NZ):
+                    sum_up(b, dest, dest - at).wait_send()
+                if at < NZ - 1:
+                    stat_up(b, ml2).wait_send()
+                for dest in range(at):
+                    sum_down(b, dest, at - dest).wait_send()
+                if at > 0:
+                    stat_down(b, ml2).wait_send()
 
 
 def attend_all(q, lens, c_kv, k_t, score_scale):
@@ -238,24 +348,28 @@
         in_specs=[pl.BlockSpec(memory_space=pltpu.SMEM)] + [pl.BlockSpec(memory_space=pl.ANY)] * 3,
         out_specs=pl.BlockSpec(memory_space=pltpu.VMEM),
         scratch_shapes=[
-            pltpu.VMEM((nb, 16, 9, 16, 128), bf16),
+            pltpu.VMEM((nb, 2, 2, 4, 9, 16, 128), bf16),
             pltpu.VMEM((slots, local_len, lat), bf16),
             pltpu.VMEM((slots, k_t.shape[1], local_len), bf16),
-            pltpu.VMEM((nb, 16, 32, lat), f32),
+            pltpu.VMEM((nb, 2, 2, 4, 32, lat), f32),
             pltpu.VMEM((nb, 2, 8, 128), f32),
             pltpu.VMEM((nb, 8, 128), f32),
             pltpu.VMEM((nb, 8, 128), f32),
-            pltpu.VMEM((nb, 8, 32, lat), f32),
+            pltpu.VMEM((nb, 2, 4, 32, lat), f32),
             pltpu.VMEM((nb, 8, 128), f32),
             pltpu.VMEM((nb, 4, 32, lat), f32),
             pltpu.VMEM((nb, 8, 128), f32),
-            pltpu.VMEM((3, nb, 32, lat), f32),
-            pltpu.VMEM((3, nb, 8, 128), f32),
+            pltpu.VMEM((nb, 4, 32, lat), f32),
+            pltpu.VMEM((nb, 8, 128), f32),
+            pltpu.VMEM((nb, 8, 128), f32),
+            pltpu.VMEM((nb, 4, 32, lat), f32),
+            pltpu.VMEM((nb, 8, 128), f32),
+            pltpu.VMEM((nb, 8, 128), f32),
             pltpu.VMEM((128, 128), f32),
             dma, dma((slots,)), dma((slots,)),
-            dma((nb, 3)), dma((nb, 3)), dma((nb,)), dma((nb,)), dma((nb,)), dma((nb,)),
-            dma((nb,)), dma((nb,)), dma((nb,)), dma((nb,)), dma((nb, 3)), dma((nb, 3)),
-            dma((nb,)), dma((nb,)), dma((nb,)), dma((nb,)), dma((nb, 3)), dma((nb, 3)),
+            dma((nb,)), dma((nb,)), dma((nb, 3)), dma((nb, 3)), dma((nb, 3)), dma((nb, 3)), dma((nb,)), dma((nb,)),
+            dma((nb, 2)), dma((nb, 2)), dma((nb,)), dma((nb,)), dma((nb, 3)), dma((nb, 3)), dma((nb, 3)), dma((nb, 3)),
+            dma((nb,)), dma((nb,)), dma((nb,)), dma((nb,)), dma((nb,)), dma((nb,)), dma((nb,)), dma((nb,)),
         ],
         compiler_params=pltpu.CompilerParams(
             collective_id=0, has_side_effects=True, vmem_limit_bytes=64 * 1024 * 1024 - 65536),

time: 247 us -> 213 us (0.86)
  Pallas kernels: 215 us -> 183 us
    pallas_call x1, Pallas kernels: 173 us -> 142 us  [attend_all(): pl.pallas_call(functools.partial(attend_kernel, score_scale * math.log2(m...]
where the time goes in v2:
time: 213 us
  Pallas kernels  183 us (86%)
  matrix products  22.8 us (11%)
  local copies, waits for them, and re-layouts  5.87 us (3%)
    pallas_call x1, Pallas kernels, attend_all(): pl.pallas_call(functools.partial(attend_kernel, score_scale * math.log2(m...  142 us
    pallas_call x1, Pallas kernels, total_all(): pl.pallas_call(total_kernel, out_shape=jax.ShapeDtypeStruct((n, dim), bf1...  41.2 us
    dot_general x1, matrix products, local_step(): jnp.einsum('bqhk,hkc->bqhc', q_nope, w_uk, preferred_element_type=f32)  8.5 us
    dot_general x1, matrix products, local_step(): y_part = jnp.einsum('niw,iwe->ne', o_val, w_o, preferred_element_type=f32)  7.3 us
    dot_general x1, matrix products, local_step(): jnp.einsum('cre,eis->cris', hidden, w_qr, preferred_element_type=f32)  6.99 us

profile of v2, /device:TPU:1, one launch (start us, length us, event | category | flops | bytes accessed | tf_op | source)
XLA Modules:
  0.0 212.7 jit_solution(6491561705078962553)
XLA Ops:
  0.0 7.0 %fusion.5 = bf16[16,4,8,64]{3,0,2,1:T(8,128)(2,1)S(1)} fusion(bf16[7168,8,64]{0,2,1:T(8,128)(2,1)} %param.14, bf16[16,4,7168,1]{2,1,0,3:T(4,128)(2,1)} %bitcast.37), kind=kOutput, calls=%fused_computation.7 | convolution fusion | flops 469794816 | bytes 8323072 | tf_op jit(solution)/shard_map/cre,eis->cris/dot_general | solution.py:454
  7.0 0.1 copy.39
  7.1 0.1 reshape.24
  7.3 8.5 %fusion.4 = bf16[16,4,8,512]{3,0,1,2:T(8,128)(2,1)S(1)} fusion(bf16[8,128,512]{2,1,0:T(8,128)(2,1)} %param.15, bf16[7168,8,128,1]{2,1,0,3:T(8,128)(2,1)} %bitcast.41, bf16[16,4,7168,1]{2,1,0,3:T(4,128)(2,1)} %bitcast.38), kind=kOutput, calls=%fused_computation.6 | convolution fusion | flops 1006960640 | bytes 17170432 | tf_op jit(solution)/shard_map/bqhk,hkc->bqhc/dot_general | solution.py:455
  15.8 0.3 copy.12
  16.1 0.1 reshape.21
  16.2 0.1 copy.13
  16.3 0.9 pad_maximum_fusion.q_hbm
  17.2 141.9 %attend_all.1 = bf16[16,32,512]{2,1,0:T(8,128)(2,1)} custom-call(s32[16]{0:T(128)} %lens.1, bf16[16,9,16,128]{3,2,1,0:T(8,128)(2,1)} %pad_maximum_fusion.q_hbm, bf16[16,1024,512]{2,1,0:T(8,128)(2,1)} %c_hbm.1, bf16[16,64,1024]{2,1,0:T(8,128)(2,1)} %bitcast.33), custom_call_target="tpu_custom_call" | custom-call | tf_op jit(solution)/shard_map/attend_all/pallas_call | solution.py:345
  159.1 1.7 reshape.26.h_ref
  160.7 7.3 %convolution_bitcast_fusion.y_ref = f32[64,7168]{1,0:T(8,128)S(1)} fusion(bf16[8,128,7168]{2,1,0:T(8,128)(2,1)} %param.17, bf16[8,512,128]{2,1,0:T(8,128)(2,1)} %param.16, bf16[64,8,512]{2,1,0:T(8,128)(2,1)} %bitcast.34), kind=kOutput, calls=%fused_computation.2 | convolution fusion | flops 1006698496 | bytes 18087936 | tf_op jit(solution)/shard_map/niw,iwe->ne/dot_general | solution.py:462
  168.0 41.2 %total_all.1 = bf16[64,7168]{1,0:T(8,128)(2,1)S(1)} custom-call(f32[64,7168]{1,0:T(8,128)S(1)} %convolution_bitcast_fusion.y_ref, bf16[64,7168]{1,0:T(8,128)(2,1)S(1)} %reshape.26.h_ref), custom_call_target="tpu_custom_call" | custom-call | tf_op jit(solution)/shard_map/total_all/pallas_call | solution.py:432
  209.3 0.0 copy-start
  209.3 0.9 copy-done
  210.2 2.5 %reshape.27 = bf16[16,4,7168]{2,1,0:T(4,128)(2,1)} reshape(bf16[64,7168]{1,0:T(8,128)(2,1)} %copy-done) | data formatting | bytes 1835008 | tf_op jit(solution)/shard_map/reshape | solution.py:463
Async XLA Ops:
  209.3 0.9 copy-start

commit v3 on v2

--- a/solution.py
+++ b/solution.py
@@ -41,7 +41,7 @@
     return jnp.concatenate([rows, pad], axis=0).T
 
 
-def attend_kernel(scale, lens, q_hbm, c_hbm, k_hbm, out,
+def attend_kernel(scale, lens, q_hbm, c_hbm, k_hbm, wuv, out,
                   qbuf, ck, kr, o_full, ml0, ml1, ml2, rc_c, ml_c, rc_y, ml_y,
                   rc_u, ml_u, ml_us, rc_d, ml_d, ml_ds, wcol,
                   q_sem, c_sem, k_sem,
@@ -281,10 +281,17 @@
         wcol[...] = merge_stats(parts, True)[1]
         cols = wcol[pl.ds(pl.multiple_of(y * 64 + at * 16, 16), 16), :]
         n = len(parts)
+        halves = []
         for hf in range(2):
             rows = pl.ds(hf * 16, 16)
             o = sum(part[rows, :] * cols[:, n * hf + j:n * hf + j + 1] for j, part in enumerate(sums))
-            out[b, rows, :] = o.astype(bf16)
+            halves.append(o.astype(bf16))
+        o = jnp.concatenate(halves, axis=0)
+        head = lax.rem(lax.broadcasted_iota(jnp.int32, (32, 128), 0), 8)
+        for h in range(8):
+            v = jnp.dot(o, wuv[h], preferred_element_type=f32)
+            v = jnp.where(head == h, v, 0.0).reshape(4, 8, 128).sum(axis=1)
+            out[b, :, h * 128:(h + 1) * 128] = v.astype(bf16)
 
     def step_f(b):
         for at in range(NZ):
@@ -338,14 +345,15 @@
                     stat_down(b, ml2).wait_send()
 
 
-def attend_all(q, lens, c_kv, k_t, score_scale):
+def attend_all(q, lens, c_kv, k_t, w_uv, score_scale):
     nb, local_len, lat = c_kv.shape
     slots = 3
     dma = pltpu.SemaphoreType.DMA
     return pl.pallas_call(
         functools.partial(attend_kernel, score_scale * math.log2(math.e)),
-        out_shape=jax.ShapeDtypeStruct((nb, 32, lat), bf16),
-        in_specs=[pl.BlockSpec(memory_space=pltpu.SMEM)] + [pl.BlockSpec(memory_space=pl.ANY)] * 3,
+        out_shape=jax.ShapeDtypeStruct((nb, 4, w_uv.shape[0] * w_uv.shape[2]), bf16),
+        in_specs=[pl.BlockSpec(memory_space=pltpu.SMEM)] + [pl.BlockSpec(memory_space=pl.ANY)] * 3
+        + [pl.BlockSpec(memory_space=pltpu.VMEM)],
         out_specs=pl.BlockSpec(memory_space=pltpu.VMEM),
         scratch_shapes=[
             pltpu.VMEM((nb, 2, 2, 4, 9, 16, 128), bf16),
@@ -374,75 +382,152 @@
         compiler_params=pltpu.CompilerParams(
             collective_id=0, has_side_effects=True, vmem_limit_bytes=64 * 1024 * 1024 - 65536),
         name="attend_all",
-    )(lens, q, c_kv, k_t)
-
-
-def total_kernel(y_ref, h_ref, out, acc, rc1, rc2, gat, s1, r1, s2, r2, s3, r3, s4, r4):
+    )(lens, q, c_kv, k_t, w_uv)
+
+
+def total_kernel(ov_ref, w_hbm, h_hbm, out, wbuf, hbuf, part, gat, rc_c, rc_y, rc_z,
+                 w_sem, h_sem, sc_s, sc_r, sy_s, sy_r, sz_s, sz_r, gz_s, gz_r, gy_s, gy_r, gc_s, gc_r):
     _, z, y, c = place()
-    rows, half = y_ref.shape[0], y_ref.shape[1] // 2
-    wide, deep = half // NY, rows // NZ
-    core_peer = seq_of(z, y, 1 - c)
-    me = z * NY + y
-    tos = [lax.rem(me + d, 8) for d in range(1, 8)]
-    froms = [lax.rem(me + 8 - d, 8) for d in range(1, 8)]
-    meet([core_peer] + [t * NC + c for t in tos])
-
-    def lanes(cc):
-        return pl.ds(pl.multiple_of(cc * half, 128), half)
-
-    swap = remote(y_ref.at[:, lanes(1 - c)], rc1, s1, r1, core_peer)
-    swap.start()
-    swap.wait_recv()
-    acc[...] = y_ref[:, lanes(c)] + rc1[...]
-
-    def piece(chip):
-        return pl.ds((chip // NY) * deep, deep), pl.ds(pl.multiple_of((chip % NY) * wide, 128), wide)
-
-    def out_piece(chip):
-        return pl.ds((chip // NY) * deep, deep), pl.ds(pl.multiple_of(c * half + (chip % NY) * wide, 128), wide)
-
-    first = [remote(acc.at[piece(tos[d])], rc2.at[d], s2.at[d], r2.at[d], tos[d] * NC + c) for d in range(7)]
-    for cp in first:
-        cp.start()
-    for cp in first:
-        cp.wait_recv()
-    total = acc[piece(me)]
-    for d in range(7):
-        total = total + rc2[d]
-    gat[out_piece(me)] = (h_ref[out_piece(me)].astype(f32) + total).astype(bf16)
-    second = [remote(gat.at[out_piece(me)], gat.at[out_piece(me)], s3.at[d], r3.at[d], tos[d] * NC + c) for d in range(7)]
-    for cp in second:
-        cp.start()
-    for d in range(7):
-        blk = gat.at[out_piece(froms[d])]
-        remote(blk, blk, s3.at[d], r3.at[d], tos[d] * NC + c).wait_recv()
-    last = remote(gat.at[:, lanes(c)], gat.at[:, lanes(c)], s4, r4, core_peer)
-    last.start()
-    other = gat.at[:, lanes(1 - c)]
-    remote(other, other, s4, r4, core_peer).wait_recv()
-    out[...] = gat[...]
-    for cp in [swap, last] + first + second:
-        cp.wait_send()
-
-
-def total_all(y_part, hidden):
-    n, dim = y_part.shape
+    chunks, lanes = wbuf.shape[0], wbuf.shape[4]
+    deep = part.shape[3] // NZ
+    core_peer, y_peer = seq_of(z, y, 1 - c), seq_of(z, 1 - y, c)
+    zs = [lax.rem(z + d, NZ) for d in (1, 2, 3)]
+    zf = [lax.rem(z + NZ - d, NZ) for d in (1, 2, 3)]
+
+    def where(cc, yy, k):
+        return pl.ds(pl.multiple_of((cc * NY + yy) * (chunks * lanes) + k * lanes, 128), lanes)
+
+    def weights(k):
+        return [pltpu.make_async_copy(w_hbm.at[:, where(cc, yy, k)], wbuf.at[k, cc, yy], w_sem.at[k, cc * 2 + yy])
+                for cc in range(2) for yy in range(2)]
+
+    for k in range(chunks):
+        for cp in weights(k):
+            cp.start()
+    nb = h_hbm.shape[0]
+    own_h = pltpu.make_async_copy(
+        h_hbm.at[pl.ds(z * (nb // NZ), nb // NZ), :, pl.ds(pl.multiple_of((c * NY + y) * (chunks * lanes), 128), chunks * lanes)],
+        hbuf, h_sem)
+    own_h.start()
+    meet([core_peer, y_peer] + [seq_of(p, y, c) for p in zs])
+    own_h.wait()
+
+    def band(at):
+        return pl.ds(pl.multiple_of(at * deep, deep), deep)
+
+    def sum_c(k):
+        return remote(part.at[k, 1 - c], rc_c.at[k], sc_s.at[k], sc_r.at[k], core_peer)
+
+    def sum_y(k):
+        return remote(part.at[k, c, 1 - y], rc_y.at[k], sy_s.at[k], sy_r.at[k], y_peer)
+
+    def sum_z(k, d):
+        return remote(part.at[k, c, y, band(zs[d])], rc_z.at[k, d], sz_s.at[k, d], sz_r.at[k, d], seq_of(zs[d], y, c))
+
+    def give_z(k, d, at):
+        piece = gat.at[k, c, y, band(at)]
+        return remote(piece, piece, gz_s.at[k, d], gz_r.at[k, d], seq_of(zs[d], y, c))
+
+    def give_y(k, yy):
+        return remote(gat.at[k, c, yy], gat.at[k, c, yy], gy_s.at[k], gy_r.at[k], y_peer)
+
+    def give_c(k, cc):
+        return remote(gat.at[k, cc], gat.at[k, cc], gc_s.at[k], gc_r.at[k], core_peer)
+
+    def multiply(k):
+        for cp in weights(k):
+            cp.wait()
+        ov = ov_ref[...]
+        for cc in (1 - c, c):
+            for yy in range(2):
+                part[k, cc, yy] = jnp.dot(ov, wbuf[k, cc, yy], preferred_element_type=f32)
+            if cc is not c:
+                sum_c(k).start()
+
+    def step_d(k):
+        sum_c(k).wait_recv()
+        part[k, c] = part[k, c] + rc_c[k]
+        sum_y(k).start()
+
+    def step_e(k):
+        sum_y(k).wait_recv()
+        part[k, c, y] = part[k, c, y] + rc_y[k]
+        for d in range(3):
+            sum_z(k, d).start()
+
+    def step_f(k):
+        for d in range(3):
+            sum_z(k, d).wait_recv()
+        total = part[k, c, y, band(z)] + rc_z[k, 0] + rc_z[k, 1] + rc_z[k, 2]
+        own = hbuf[:, :, pl.ds(pl.multiple_of(k * lanes, 128), lanes)].astype(f32).reshape(deep, lanes)
+        gat[k, c, y, band(z)] = (own + total).astype(bf16)
+        for d in range(3):
+            give_z(k, d, z).start()
+
+    def step_h(k):
+        for d in range(3):
+            give_z(k, d, zf[d]).wait_recv()
+        give_y(k, y).start()
+
+    def step_i(k):
+        give_y(k, 1 - y).wait_recv()
+        give_c(k, c).start()
+
+    def step_j(k):
+        give_c(k, 1 - c).wait_recv()
+        for cc in range(2):
+            for yy in range(2):
+                out[:, :, where(cc, yy, k)] = gat[k, cc, yy].astype(f32).reshape(nb, -1, lanes).astype(bf16)
+
+    steps = ((10, step_j), (9, step_i), (7, step_h), (5, step_f), (3, step_e), (1, step_d), (0, multiply))
+
+    @pl.loop(0, chunks + 10)
+    def _(it):
+        for lag, fn in steps:
+            k = it - lag
+
+            @pl.when((k >= 0) & (k < chunks))
+            def _(fn=fn, k=k):
+                fn(k)
+
+    @pl.loop(0, chunks)
+    def _(k):
+        sum_c(k).wait_send()
+        sum_y(k).wait_send()
+        for d in range(3):
+            sum_z(k, d).wait_send()
+            give_z(k, d, z).wait_send()
+        give_y(k, y).wait_send()
+        give_c(k, c).wait_send()
+
+
+def total_all(ov, w_o, hidden):
+    n, dim = ov.shape[0], w_o.shape[1]
+    nb, nq, _ = hidden.shape
+    chunks = next(k for k in (7, 1) if dim % (4 * k * 128) == 0)
+    lanes = dim // (4 * chunks)
     dma = pltpu.SemaphoreType.DMA
-    vm = pl.BlockSpec(memory_space=pltpu.VMEM)
+    vm, hbm = pl.BlockSpec(memory_space=pltpu.VMEM), pl.BlockSpec(memory_space=pl.ANY)
+    one, three = dma((chunks,)), dma((chunks, 3))
     return pl.pallas_call(
         total_kernel,
-        out_shape=jax.ShapeDtypeStruct((n, dim), bf16),
-        in_specs=[vm, vm],
+        out_shape=jax.ShapeDtypeStruct((nb, nq, dim), bf16),
+        in_specs=[vm, hbm, hbm],
         out_specs=vm,
         scratch_shapes=[
-            pltpu.VMEM((n, dim // 2), f32), pltpu.VMEM((n, dim // 2), f32),
-            pltpu.VMEM((7, n // NZ, dim // 4), f32), pltpu.VMEM((n, dim), bf16),
-            dma, dma, dma((7,)), dma((7,)), dma((7,)), dma((7,)), dma, dma,
+            pltpu.VMEM((chunks, 2, 2, w_o.shape[0], lanes), bf16),
+            pltpu.VMEM((nb // NZ, nq, chunks * lanes), bf16),
+            pltpu.VMEM((chunks, 2, 2, n, lanes), f32),
+            pltpu.VMEM((chunks, 2, 2, n, lanes), bf16),
+            pltpu.VMEM((chunks, 2, n, lanes), f32),
+            pltpu.VMEM((chunks, n, lanes), f32),
+            pltpu.VMEM((chunks, 3, n // NZ, lanes), f32),
+            dma((chunks, 4)), dma, one, one, one, one, three, three, three, three, one, one, one, one,
         ],
         compiler_params=pltpu.CompilerParams(
-            collective_id=1, has_side_effects=True, vmem_limit_bytes=32 * 1024 * 1024),
+            collective_id=1, has_side_effects=True, vmem_limit_bytes=40 * 1024 * 1024),
         name="total_all",
-    )(y_part, hidden)
+    )(ov, w_o, hidden)
 
 
 def solution(mesh):
@@ -456,11 +541,8 @@
         q_a = q_lat.reshape(nb, 2, 16, 4, 128).transpose(0, 1, 3, 2, 4).reshape(nb, 8, 16, 128)
         q_b = q_rope.reshape(nb, 2, 16, 64).transpose(0, 2, 1, 3).reshape(nb, 1, 16, 128)
         q = jnp.concatenate([q_a, q_b], axis=1)
-        o_lat = attend_all(q, cache_lens, c_kv, jnp.swapaxes(k_r, 1, 2), score_scale)
-        o_lat = o_lat.reshape(nb * nq, nh, lat)
-        o_val = jnp.einsum("nhc,hcv->nhv", o_lat, w_uv, preferred_element_type=f32).astype(bf16)
-        y_part = jnp.einsum("niw,iwe->ne", o_val, w_o, preferred_element_type=f32)
-        return total_all(y_part, hidden.reshape(nb * nq, dim)).reshape(nb, nq, dim)
+        o_val = attend_all(q, cache_lens, c_kv, jnp.swapaxes(k_r, 1, 2), w_uv, score_scale)
+        return total_all(o_val.reshape(nb * nq, -1), w_o.reshape(-1, dim), hidden)
 
     specs_in = (P("batch", None, None), P("batch"), P("batch", "seq", None), P("batch", "seq", None),
                 P(None, "seq", None), P(None, "seq", None), P("seq", None, None), P("seq", None, None),

time: 213 us -> 199 us (0.934)
  matrix products: 22.8 us -> 15.5 us
  Pallas kernels: 183 us -> 179 us
    dot_general x1 -> x0, matrix products: 7.3 us -> none  [local_step(): y_part = jnp.einsum('niw,iwe->ne', o_val, w_o, preferred_element_type=f32)]
    pallas_call x1, Pallas kernels: 41.2 us -> 36.3 us  [total_all(): pl.pallas_call(total_kernel, out_shape=jax.ShapeDtypeStruct((nb, nq, dim)...]
    reshape x2 -> x1, local copies, waits for them, and re-layouts: 4.18 us -> 0.94 us  [local_step(): return total_all(o_val.reshape(nb * nq, -1), w_o.reshape(-1, dim), hidden)]
where the time goes in v3:
time: 199 us
  Pallas kernels  179 us (90%)
  matrix products  15.5 us (8%)
  local copies, waits for them, and re-layouts  3.8 us (2%)
    pallas_call x1, Pallas kernels, attend_all(): pl.pallas_call(functools.partial(attend_kernel, score_scale * math.log2(m...  143 us
    pallas_call x1, Pallas kernels, total_all(): pl.pallas_call(total_kernel, out_shape=jax.ShapeDtypeStruct((nb, nq, dim)...  36.3 us
    dot_general x1, matrix products, local_step(): jnp.einsum('bqhk,hkc->bqhc', q_nope, w_uk, preferred_element_type=f32)  8.5 us
    dot_general x1, matrix products, local_step(): jnp.einsum('cre,eis->cris', hidden, w_qr, preferred_element_type=f32)  6.99 us

profile of v3, /device:TPU:1, one launch (start us, length us, event | category | flops | bytes accessed | tf_op | source)
XLA Modules:
  0.0 199.2 jit_solution(5750820795754435964)
XLA Ops:
  0.0 7.0 %fusion.5 = bf16[16,4,8,64]{3,0,2,1:T(8,128)(2,1)S(1)} fusion(bf16[7168,8,64]{0,2,1:T(8,128)(2,1)} %param.14, bf16[16,4,7168,1]{2,1,0,3:T(4,128)(2,1)} %bitcast.25), kind=kOutput, calls=%fused_computation.6 | convolution fusion | flops 469794816 | bytes 8323072 | tf_op jit(solution)/shard_map/cre,eis->cris/dot_general | solution.py:539
  7.0 0.1 copy.35
  7.1 0.1 reshape.21
  7.3 8.5 %fusion.4 = bf16[16,4,8,512]{3,0,1,2:T(8,128)(2,1)S(1)} fusion(bf16[8,128,512]{2,1,0:T(8,128)(2,1)} %param.15, bf16[7168,8,128,1]{2,1,0,3:T(8,128)(2,1)} %bitcast.33, bf16[16,4,7168,1]{2,1,0,3:T(4,128)(2,1)} %bitcast.26), kind=kOutput, calls=%fused_computation.5 | convolution fusion | flops 1006960640 | bytes 17170432 | tf_op jit(solution)/shard_map/bqhk,hkc->bqhc/dot_general | solution.py:540
  15.8 0.3 copy.12
  16.1 0.1 reshape.18
  16.2 0.1 copy.13
  16.3 0.9 pad_maximum_fusion.q_hbm
  17.2 142.6 %attend_all.1 = bf16[16,4,1024]{2,1,0:T(4,128)(2,1)} custom-call(s32[16]{0:T(128)} %lens.1, bf16[16,9,16,128]{3,2,1,0:T(8,128)(2,1)} %pad_maximum_fusion.q_hbm, bf16[16,1024,512]{2,1,0:T(8,128)(2,1)} %c_hbm.1, bf16[16,64,1024]{2,1,0:T(8,128)(2,1)} %bitcast.28, bf16[8,512,128]{2,1,0:T(8,128)(2,1)} %wuv.1), custom_call_target="tpu_custom_call" | custom-call | tf_op jit(solution)/shard_map/attend_all/pallas_call | solution.py:352
  159.8 0.9 reshape.22.ov_ref
  160.7 0.0 copy-start
  160.7 1.2 copy-done
  161.9 36.3 %total_all.1 = bf16[16,4,7168]{2,1,0:T(4,128)(2,1)S(1)} custom-call(bf16[64,1024]{1,0:T(8,128)(2,1)S(1)} %reshape.22.ov_ref, bf16[1024,7168]{1,0:T(8,128)(2,1)} %bitcast.27, bf16[16,4,7168]{2,1,0:T(4,128)(2,1)S(1)} %copy-done), custom_call_target="tpu_custom_call" | custom-call | tf_op jit(solution)/shard_map/total_all/pallas_call | solution.py:512
  198.3 0.9 copy.37
Async XLA Ops:
  160.7 1.2 copy-start

commit v4 on v3

--- a/solution.py
+++ b/solution.py
@@ -41,10 +41,10 @@
     return jnp.concatenate([rows, pad], axis=0).T
 
 
-def attend_kernel(scale, lens, q_hbm, c_hbm, k_hbm, wuv, out,
+def attend_kernel(scale, lens, q_hbm, r_hbm, c_hbm, k_hbm, h_hbm, wuv, out, h_out,
                   qbuf, ck, kr, o_full, ml0, ml1, ml2, rc_c, ml_c, rc_y, ml_y,
                   rc_u, ml_u, ml_us, rc_d, ml_d, ml_ds, wcol,
-                  q_sem, c_sem, k_sem,
+                  q_sem, h_sem, c_sem, k_sem,
                   ay_s, ay_r, au_s, au_r, ad_s, ad_r, ac_s, ac_r,
                   oc_s, oc_r, oy_s, oy_r, ou_s, ou_r, od_s, od_r,
                   mc_s, mc_r, my_s, my_r, mu_s, mu_r, md_s, md_r):
@@ -54,8 +54,10 @@
     core_peer, y_peer = seq_of(z, y, 1 - c), seq_of(z, 1 - y, c)
     upper, lower = seq_of(lax.rem(z + 1, NZ), y, c), seq_of(lax.rem(z + NZ - 1, NZ), y, c)
 
-    own_q = pltpu.make_async_copy(q_hbm, qbuf.at[:, c, y, z], q_sem)
-    own_q.start()
+    own_q = (pltpu.make_async_copy(q_hbm, qbuf.at[:, c, y, z, pl.ds(0, 8)], q_sem.at[0]),
+             pltpu.make_async_copy(r_hbm, qbuf.at[:, c, y, z, 8], q_sem.at[1]))
+    for cp in own_q:
+        cp.start()
 
     def cache(b):
         k = lax.rem(b, slots)
@@ -66,8 +68,13 @@
         for cp in cache(b):
             cp.start()
 
+    deep, wide = h_out.shape[0], h_out.shape[2]
+    own_h = pltpu.make_async_copy(
+        h_hbm.at[pl.ds(z * deep, deep), :, pl.ds(pl.multiple_of((c * NY + y) * wide, 128), wide)], h_out, h_sem)
+    own_h.start()
     meet([core_peer, y_peer, upper, lower])
-    own_q.wait()
+    for cp in own_q:
+        cp.wait()
 
     def gather_y(b, yy):
         part = qbuf.at[b, c, yy, z]
@@ -212,68 +219,58 @@
 
         @pl.when(z == 0)
         def _():
-            send_up(b, 0, ml2)
+            stat_up(b, ml2).start()
+            for dest in range(NZ - 1, 0, -1):
+                sum_up(b, dest, dest).start()
 
         @pl.when(z == NZ - 1)
         def _():
-            send_down(b, NZ - 1, ml2)
-
-    def send_up(b, at, stat):
-        for dest in range(at + 1, NZ):
-            sum_up(b, dest, dest - at).start()
-        stat_up(b, stat).start()
-
-    def send_down(b, at, stat):
-        for dest in range(at - 1, -1, -1):
-            sum_down(b, dest, at - dest).start()
-        stat_down(b, stat).start()
-
-    def recv_up(b, at, dests):
-        for dest in dests:
-            sum_up(b, dest, dest - at + 1).wait_recv()
-
-    def recv_down(b, at, dests):
-        for dest in dests:
-            sum_down(b, dest, at - dest + 1).wait_recv()
-
-    def relay(b, arrived, stat_in, stat_out, dests):
-        stats, cols = merge_stats([ml2[b, 0:4], stat_in[b, 0:4]], False)
-        stat_out[b, 0:4, :] = stats
+            stat_down(b, ml2).start()
+            for dest in range(NZ - 1):
+                sum_down(b, dest, NZ - 1 - dest).start()
+
+    def relay(b, dests, stats_in, stats_out, arrived, wait, send):
+        stats, cols = merge_stats([ml2[b, 0:4], stats_in[b, 0:4]], False)
+        stats_out[b, 0:4, :] = stats
         wcol[...] = cols
-        for dest in dests:
+        for i, dest in enumerate(dests):
+            wait(dest)
             cols = wcol[pl.ds(pl.multiple_of(y * 64 + dest * 16, 16), 16), :]
             for hf in range(2):
                 rows = pl.ds(hf * 16, 16)
                 wa, wb = (cols[:, 2 * hf + j:2 * hf + j + 1] for j in range(2))
                 o_full[b, c, y, dest, rows, :] = o_full[b, c, y, dest, rows, :] * wa + arrived[b, dest, rows, :] * wb
+            if i == 0:
+                send(None)
+            send(dest)
 
     def step_g(hop, b):
+        at = NZ - 1 - hop
+
         @pl.when(z == hop)
         def _():
+            def send(dest):
+                (stat_up(b, ml_us) if dest is None else sum_up(b, dest, dest - hop)).start()
             stat_up(b, ml2).wait_recv()
-            recv_up(b, hop, range(hop + 1, NZ))
-            relay(b, rc_u, ml_u, ml_us, range(hop + 1, NZ))
-            send_up(b, hop, ml_us)
-
-        at = NZ - 1 - hop
+            relay(b, range(NZ - 1, hop, -1), ml_u, ml_us, rc_u, lambda dest: sum_up(b, dest, dest - hop + 1).wait_recv(), send)
 
         @pl.when(z == at)
         def _():
+            def send(dest):
+                (stat_down(b, ml_ds) if dest is None else sum_down(b, dest, at - dest)).start()
             stat_down(b, ml2).wait_recv()
-            recv_down(b, at, range(at - 1, -1, -1))
-            relay(b, rc_d, ml_d, ml_ds, range(at - 1, -1, -1))
-            send_down(b, at, ml_ds)
+            relay(b, range(at), ml_d, ml_ds, rc_d, lambda dest: sum_down(b, dest, at - dest + 1).wait_recv(), send)
 
     def finish(b, at):
         parts, sums = [ml2[b, 0:4]], [o_full.at[b, c, y, at]]
         if at > 0:
-            recv_up(b, at, [at])
+            sum_up(b, at, 1).wait_recv()
             if at == NZ - 1:
                 stat_up(b, ml2).wait_recv()
             parts.append(ml_u[b, 0:4])
             sums.append(rc_u.at[b, at])
         if at < NZ - 1:
-            recv_down(b, at, [at])
+            sum_down(b, at, 1).wait_recv()
             if at == 0:
                 stat_down(b, ml2).wait_recv()
             parts.append(ml_d[b, 0:4])
@@ -314,6 +311,8 @@
             @pl.when((b >= 0) & (b < nb))
             def _(fn=fn, b=b):
                 fn(b)
+
+    own_h.wait()
 
     @pl.loop(0, nb)
     def _(b):
@@ -345,16 +344,18 @@
                     stat_down(b, ml2).wait_send()
 
 
-def attend_all(q, lens, c_kv, k_t, w_uv, score_scale):
+def attend_all(q, q_rope, lens, c_kv, k_t, hidden, w_uv, score_scale):
     nb, local_len, lat = c_kv.shape
+    nq, dim = hidden.shape[1:]
     slots = 3
     dma = pltpu.SemaphoreType.DMA
     return pl.pallas_call(
         functools.partial(attend_kernel, score_scale * math.log2(math.e)),
-        out_shape=jax.ShapeDtypeStruct((nb, 4, w_uv.shape[0] * w_uv.shape[2]), bf16),
-        in_specs=[pl.BlockSpec(memory_space=pltpu.SMEM)] + [pl.BlockSpec(memory_space=pl.ANY)] * 3
+        out_shape=(jax.ShapeDtypeStruct((nb, nq, w_uv.shape[0] * w_uv.shape[2]), bf16),
+                   jax.ShapeDtypeStruct((nb // NZ, nq, dim // 4), bf16)),
+        in_specs=[pl.BlockSpec(memory_space=pltpu.SMEM)] + [pl.BlockSpec(memory_space=pl.ANY)] * 5
         + [pl.BlockSpec(memory_space=pltpu.VMEM)],
-        out_specs=pl.BlockSpec(memory_space=pltpu.VMEM),
+        out_specs=(pl.BlockSpec(memory_space=pltpu.VMEM), pl.BlockSpec(memory_space=pltpu.VMEM)),
         scratch_shapes=[
             pltpu.VMEM((nb, 2, 2, 4, 9, 16, 128), bf16),
             pltpu.VMEM((slots, local_len, lat), bf16),
@@ -374,7 +375,7 @@
             pltpu.VMEM((nb, 8, 128), f32),
             pltpu.VMEM((nb, 8, 128), f32),
             pltpu.VMEM((128, 128), f32),
-            dma, dma((slots,)), dma((slots,)),
+            dma((2,)), dma, dma((slots,)), dma((slots,)),
             dma((nb,)), dma((nb,)), dma((nb, 3)), dma((nb, 3)), dma((nb, 3)), dma((nb, 3)), dma((nb,)), dma((nb,)),
             dma((nb, 2)), dma((nb, 2)), dma((nb,)), dma((nb,)), dma((nb, 3)), dma((nb, 3)), dma((nb, 3)), dma((nb, 3)),
             dma((nb,)), dma((nb,)), dma((nb,)), dma((nb,)), dma((nb,)), dma((nb,)), dma((nb,)), dma((nb,)),
@@ -382,11 +383,49 @@
         compiler_params=pltpu.CompilerParams(
             collective_id=0, has_side_effects=True, vmem_limit_bytes=64 * 1024 * 1024 - 65536),
         name="attend_all",
-    )(lens, q, c_kv, k_t, w_uv)
-
-
-def total_kernel(ov_ref, w_hbm, h_hbm, out, wbuf, hbuf, part, gat, rc_c, rc_y, rc_z,
-                 w_sem, h_sem, sc_s, sc_r, sy_s, sy_r, sz_s, sz_r, gz_s, gz_r, gy_s, gy_r, gc_s, gc_r):
+    )(lens, q, q_rope, c_kv, k_t, hidden, w_uv)
+
+
+def rope_kernel(h_ref, w_ref, out, acc, rows):
+    step = pl.program_id(0)
+    nb, nq, lanes = h_ref.shape
+    h = h_ref[...].astype(f32).reshape(nb * nq, lanes).astype(bf16)
+    part = lax.dot_general(h, w_ref[...], (((1,), (1,)), ((), ())), preferred_element_type=f32)
+
+    @pl.when(step == 0)
+    def _():
+        acc[...] = part
+
+    @pl.when(step > 0)
+    def _():
+        acc[...] += part
+
+    @pl.when(step == pl.num_programs(0) - 1)
+    def _():
+        for h in range(8):
+            rows[:, h, :] = acc[:, h * 64:(h + 1) * 64]
+        pairs = rows[...].reshape(nb, 2, 16, 64)
+        out[...] = jnp.concatenate([pairs[:, 0], pairs[:, 1]], axis=-1).astype(bf16)
+
+
+def rope_queries(hidden, w_t):
+    nb, nq, dim = hidden.shape
+    wide = w_t.shape[0]
+    steps = next(k for k in (7, 4, 1) if dim % (k * 128) == 0)
+    return pl.pallas_call(
+        rope_kernel,
+        grid=(steps,),
+        out_shape=jax.ShapeDtypeStruct((nb, 16, 128), bf16),
+        in_specs=[pl.BlockSpec((nb, nq, dim // steps), lambda i: (0, 0, i)), pl.BlockSpec((wide, dim // steps), lambda i: (0, i))],
+        out_specs=pl.BlockSpec((nb, 16, 128), lambda i: (0, 0, 0)),
+        scratch_shapes=[pltpu.VMEM((nb * nq, wide), f32), pltpu.VMEM((nb * nq, 8, 64), f32)],
+        compiler_params=pltpu.CompilerParams(dimension_semantics=("arbitrary",)),
+        name="rope_queries",
+    )(hidden, w_t)
+
+
+def total_kernel(ov_ref, w_hbm, hbuf, out, ov_rows, wbuf, part, gat, rc_c, rc_y, rc_z,
+                 w_sem, sc_s, sc_r, sy_s, sy_r, sz_s, sz_r, gz_s, gz_r, gy_s, gy_r, gc_s, gc_r):
     _, z, y, c = place()
     chunks, lanes = wbuf.shape[0], wbuf.shape[4]
     deep = part.shape[3] // NZ
@@ -404,13 +443,9 @@
     for k in range(chunks):
         for cp in weights(k):
             cp.start()
-    nb = h_hbm.shape[0]
-    own_h = pltpu.make_async_copy(
-        h_hbm.at[pl.ds(z * (nb // NZ), nb // NZ), :, pl.ds(pl.multiple_of((c * NY + y) * (chunks * lanes), 128), chunks * lanes)],
-        hbuf, h_sem)
-    own_h.start()
+    nb = ov_ref.shape[0]
+    ov_rows[...] = ov_ref[...].astype(f32).reshape(ov_rows.shape).astype(bf16)
     meet([core_peer, y_peer] + [seq_of(p, y, c) for p in zs])
-    own_h.wait()
 
     def band(at):
         return pl.ds(pl.multiple_of(at * deep, deep), deep)
@@ -437,7 +472,7 @@
     def multiply(k):
         for cp in weights(k):
             cp.wait()
-        ov = ov_ref[...]
+        ov = ov_rows[...]
         for cc in (1 - c, c):
             for yy in range(2):
                 part[k, cc, yy] = jnp.dot(ov, wbuf[k, cc, yy], preferred_element_type=f32)
@@ -501,9 +536,9 @@
         give_c(k, c).wait_send()
 
 
-def total_all(ov, w_o, hidden):
-    n, dim = ov.shape[0], w_o.shape[1]
-    nb, nq, _ = hidden.shape
+def total_all(ov, w_o, own_h):
+    (nb, nq, _), dim = ov.shape, w_o.shape[1]
+    n = nb * nq
     chunks = next(k for k in (7, 1) if dim % (4 * k * 128) == 0)
     lanes = dim // (4 * chunks)
     dma = pltpu.SemaphoreType.DMA
@@ -512,22 +547,22 @@
     return pl.pallas_call(
         total_kernel,
         out_shape=jax.ShapeDtypeStruct((nb, nq, dim), bf16),
-        in_specs=[vm, hbm, hbm],
+        in_specs=[vm, hbm, vm],
         out_specs=vm,
         scratch_shapes=[
+            pltpu.VMEM((n, w_o.shape[0]), bf16),
             pltpu.VMEM((chunks, 2, 2, w_o.shape[0], lanes), bf16),
-            pltpu.VMEM((nb // NZ, nq, chunks * lanes), bf16),
             pltpu.VMEM((chunks, 2, 2, n, lanes), f32),
             pltpu.VMEM((chunks, 2, 2, n, lanes), bf16),
             pltpu.VMEM((chunks, 2, n, lanes), f32),
             pltpu.VMEM((chunks, n, lanes), f32),
             pltpu.VMEM((chunks, 3, n // NZ, lanes), f32),
-            dma((chunks, 4)), dma, one, one, one, one, three, three, three, three, one, one, one, one,
+            dma((chunks, 4)), one, one, one, one, three, three, three, three, one, one, one, one,
         ],
         compiler_params=pltpu.CompilerParams(
             collective_id=1, has_side_effects=True, vmem_limit_bytes=40 * 1024 * 1024),
         name="total_all",
-    )(ov, w_o, hidden)
+    )(ov, w_o, own_h)
 
 
 def solution(mesh):
@@ -536,13 +571,11 @@
         nb, nq, dim = hidden.shape
         nh, lat = w_uk.shape[0], w_uk.shape[2]
         q_nope = jnp.einsum("cre,eil->cril", hidden, w_uq, preferred_element_type=f32).astype(bf16)
-        q_rope = jnp.einsum("cre,eis->cris", hidden, w_qr, preferred_element_type=f32).astype(bf16)
         q_lat = jnp.einsum("bqhk,hkc->bqhc", q_nope, w_uk, preferred_element_type=f32).astype(bf16)
-        q_a = q_lat.reshape(nb, 2, 16, 4, 128).transpose(0, 1, 3, 2, 4).reshape(nb, 8, 16, 128)
-        q_b = q_rope.reshape(nb, 2, 16, 64).transpose(0, 2, 1, 3).reshape(nb, 1, 16, 128)
-        q = jnp.concatenate([q_a, q_b], axis=1)
-        o_val = attend_all(q, cache_lens, c_kv, jnp.swapaxes(k_r, 1, 2), w_uv, score_scale)
-        return total_all(o_val.reshape(nb * nq, -1), w_o.reshape(-1, dim), hidden)
+        q = q_lat.reshape(nb, 2, 16, 4, 128).transpose(0, 1, 3, 2, 4).reshape(nb, 8, 16, 128)
+        q_rope = rope_queries(hidden, w_qr.transpose(1, 2, 0).reshape(-1, dim))
+        o_val, own_h = attend_all(q, q_rope, cache_lens, c_kv, jnp.swapaxes(k_r, 1, 2), hidden, w_uv, score_scale)
+        return total_all(o_val, w_o.reshape(-1, dim), own_h)
 
     specs_in = (P("batch", None, None), P("batch"), P("batch", "seq", None), P("batch", "seq", None),
                 P(None, "seq", None), P(None, "seq", None), P("seq", None, None), P("seq", None, None),

time: 199 us -> 198 us (level)
  matrix products: 15.5 us -> 8.5 us
  Pallas kernels: 179 us -> 185 us
    pallas_call x0 -> x1, Pallas kernels: none -> 8.09 us  [rope_queries(): pl.pallas_call(rope_kernel, grid=(steps,), out_shape=jax.ShapeDtypeStruct...]
    dot_general x1 -> x0, matrix products: 6.99 us -> none  [local_step(): jnp.einsum('cre,eis->cris', hidden, w_qr, preferred_element_type=f32)]
    pallas_call x1, Pallas kernels: 143 us -> 140 us  [attend_all(): pl.pallas_call(functools.partial(attend_kernel, score_scale * math.log2(m...]
where the time goes in v4:
time: 198 us; the launch traced here: 197 us
  Pallas kernels  185 us (93%)
  matrix products  8.5 us (4%)
  local copies, waits for them, and re-layouts  3.96 us (2%)
    pallas_call x1, Pallas kernels, attend_all(): pl.pallas_call(functools.partial(attend_kernel, score_scale * math.log2(m...  140 us
    pallas_call x1, Pallas kernels, total_all(): pl.pallas_call(total_kernel, out_shape=jax.ShapeDtypeStruct((nb, nq, dim)...  36.5 us
    dot_general x1, matrix products, local_step(): jnp.einsum('bqhk,hkc->bqhc', q_nope, w_uk, preferred_element_type=f32)  8.5 us
    pallas_call x1, Pallas kernels, rope_queries(): pl.pallas_call(rope_kernel, grid=(steps,), out_shape=jax.ShapeDtypeStruct...  8.09 us

profile of v4, /device:TPU:1, one launch (start us, length us, event | category | flops | bytes accessed | tf_op | source)
XLA Modules:
  0.0 197.3 jit_solution(10110829683621131098)
XLA Ops:
  0.0 8.1 %rope_queries.1.r_hbm = bf16[16,16,128]{2,1,0:T(8,128)(2,1)} custom-call(bf16[16,4,7168]{2,1,0:T(4,128)(2,1)} %h_hbm.1, bf16[512,7168]{1,0:T(8,128)(2,1)} %bitcast.19), custom_call_target="tpu_custom_call" | custom-call | tf_op jit(solution)/shard_map/rope_queries/pallas_call | solution.py:415
  8.1 8.5 %fusion.2 = bf16[16,4,8,512]{3,0,1,2:T(8,128)(2,1)S(1)} fusion(bf16[8,128,512]{2,1,0:T(8,128)(2,1)} %param.15, bf16[7168,8,128,1]{2,1,0,3:T(8,128)(2,1)} %bitcast.24, bf16[16,4,7168,1]{2,1,0,3:T(4,128)(2,1)} %bitcast.20), kind=kOutput, calls=%fused_computation.3 | convolution fusion | flops 1006960640 | bytes 17170432 | tf_op jit(solution)/shard_map/bqhk,hkc->bqhc/dot_general | solution.py:574
  16.6 0.3 copy.10
  16.9 0.1 reshape.12
  17.0 0.9 copy.11
  17.9 140.2 %attend_all.1 = (bf16[16,4,1024]{2,1,0:T(4,128)(2,1)}, bf16[4,4,1792]{2,1,0:T(4,128)(2,1)}) custom-call(s32[16]{0:T(128)} %lens.1, bf16[16,8,16,128]{3,2,1,0:T(8,128)(2,1)} %bitcast.22, bf16[16,16,128]{2,1,0:T(8,128)(2,1)} %rope_queries.1.r_hbm, bf16[16,1024,512]{2,1,0:T(8,128)(2,1)} %c_hbm.1, bf16[16,64,1024]{2,1,0:T(8,128)(2,1)} %bitcast.21, ...), custom_call_target="tpu_custom_call" | custom-call | tf_op jit(solution)/shard_map/attend_all/pallas_call | solution.py:352
  158.2 0.0 copy-start
  158.2 0.9 copy-done
  159.1 0.0 copy-start.1
  159.1 0.8 copy-done.1
  159.9 36.5 %total_all.1 = bf16[16,4,7168]{2,1,0:T(4,128)(2,1)S(1)} custom-call(bf16[16,4,1024]{2,1,0:T(4,128)(2,1)S(1)} %copy-done, bf16[1024,7168]{1,0:T(8,128)(2,1)} %bitcast.18, bf16[4,4,1792]{2,1,0:T(4,128)(2,1)S(1)} %copy-done.1), custom_call_target="tpu_custom_call" | custom-call | tf_op jit(solution)/shard_map/total_all/pallas_call | solution.py:547
  196.4 0.9 copy.26
Async XLA Ops:
  158.2 0.9 copy-start
  159.1 0.8 copy-start.1

commit v5 on v4

--- a/solution.py
+++ b/solution.py
@@ -72,7 +72,7 @@
     own_h = pltpu.make_async_copy(
         h_hbm.at[pl.ds(z * deep, deep), :, pl.ds(pl.multiple_of((c * NY + y) * wide, 128), wide)], h_out, h_sem)
     own_h.start()
-    meet([core_peer, y_peer, upper, lower])
+    meet([core_peer, y_peer] + [seq_of(lax.rem(z + d, NZ), y, c) for d in (1, 2, 3)])
     for cp in own_q:
         cp.wait()
 
@@ -133,17 +133,44 @@
         def _():
             gather_down(b, z + d, d).wait_recv()
 
+    direct = 1
+
+    def straight(b, d, go):
+        part = qbuf.at[b, c, :, z]
+
+        @pl.when(z + d < NZ)
+        def _():
+            go(remote(part, part, au_s.at[b, d - 1], au_r.at[b, d - 1], seq_of(lax.rem(z + d, NZ), y, c)))
+
+        @pl.when(z - d >= 0)
+        def _():
+            go(remote(part, part, ad_s.at[b, d - 1], ad_r.at[b, d - 1], seq_of(lax.rem(z + NZ - d, NZ), y, c)))
+
     def step_z1(b):
         gather_y(b, 1 - y).wait_recv()
-        pass_on(b, 1)
+
+        @pl.when(b < direct)
+        def _():
+            for d in (3, 2, 1):
+                straight(b, d, lambda cp: cp.start())
+
+        @pl.when(b >= direct)
+        def _():
+            pass_on(b, 1)
 
     def step_z2(b):
         arrive(b, 1)
-        pass_on(b, 2)
+
+        @pl.when(b >= direct)
+        def _():
+            pass_on(b, 2)
 
     def step_z3(b):
         arrive(b, 2)
-        pass_on(b, 3)
+
+        @pl.when(b >= direct)
+        def _():
+            pass_on(b, 3)
 
     def step_z4(b):
         arrive(b, 3)
@@ -318,14 +345,21 @@
     def _(b):
         gather_y(b, y).wait_send()
         gather_c(b, c).wait_send()
-        for d in (1, 2, 3):
-            @pl.when((z < NZ - 1) & (z - (d - 1) >= 0))
-            def _(d=d):
-                gather_up(b, z - (d - 1), d).wait_send()
-
-            @pl.when((z > 0) & (z + (d - 1) < NZ))
-            def _(d=d):
-                gather_down(b, z + (d - 1), d).wait_send()
+        @pl.when(b < direct)
+        def _():
+            for d in (1, 2, 3):
+                straight(b, d, lambda cp: cp.wait_send())
+
+        @pl.when(b >= direct)
+        def _():
+            for d in (1, 2, 3):
+                @pl.when((z < NZ - 1) & (z - (d - 1) >= 0))
+                def _(d=d):
+                    gather_up(b, z - (d - 1), d).wait_send()
+
+                @pl.when((z > 0) & (z + (d - 1) < NZ))
+                def _(d=d):
+                    gather_down(b, z + (d - 1), d).wait_send()
         sum_c(b, 0).wait_send()
         sum_c(b, 1).wait_send()
         stat_c(b).wait_send()
@@ -390,7 +424,7 @@
     step = pl.program_id(0)
     nb, nq, lanes = h_ref.shape
     h = h_ref[...].astype(f32).reshape(nb * nq, lanes).astype(bf16)
-    part = lax.dot_general(h, w_ref[...], (((1,), (1,)), ((), ())), preferred_element_type=f32)
+    part = lax.dot_general(w_ref[...], h, (((1,), (1,)), ((), ())), preferred_element_type=f32)
 
     @pl.when(step == 0)
     def _():
@@ -403,7 +437,7 @@
     @pl.when(step == pl.num_programs(0) - 1)
     def _():
         for h in range(8):
-            rows[:, h, :] = acc[:, h * 64:(h + 1) * 64]
+            rows[:, h, :] = acc[h * 64:(h + 1) * 64, :].T
         pairs = rows[...].reshape(nb, 2, 16, 64)
         out[...] = jnp.concatenate([pairs[:, 0], pairs[:, 1]], axis=-1).astype(bf16)
 
@@ -418,14 +452,14 @@
         out_shape=jax.ShapeDtypeStruct((nb, 16, 128), bf16),
         in_specs=[pl.BlockSpec((nb, nq, dim // steps), lambda i: (0, 0, i)), pl.BlockSpec((wide, dim // steps), lambda i: (0, i))],
         out_specs=pl.BlockSpec((nb, 16, 128), lambda i: (0, 0, 0)),
-        scratch_shapes=[pltpu.VMEM((nb * nq, wide), f32), pltpu.VMEM((nb * nq, 8, 64), f32)],
+        scratch_shapes=[pltpu.VMEM((wide, nb * nq), f32), pltpu.VMEM((nb * nq, 8, 64), f32)],
         compiler_params=pltpu.CompilerParams(dimension_semantics=("arbitrary",)),
         name="rope_queries",
     )(hidden, w_t)
 
 
-def total_kernel(ov_ref, w_hbm, hbuf, out, ov_rows, wbuf, part, gat, rc_c, rc_y, rc_z,
-                 w_sem, sc_s, sc_r, sy_s, sy_r, sz_s, sz_r, gz_s, gz_r, gy_s, gy_r, gc_s, gc_r):
+def total_kernel(ov_hbm, w_hbm, h_hbm, out, ov_ref, hbuf, ov_rows, wbuf, part, gat, rc_c, rc_y, rc_z,
+                 in_sem, w_sem, sc_s, sc_r, sy_s, sy_r, sz_s, sz_r, gz_s, gz_r, gy_s, gy_r, gc_s, gc_r):
     _, z, y, c = place()
     chunks, lanes = wbuf.shape[0], wbuf.shape[4]
     deep = part.shape[3] // NZ
@@ -440,10 +474,15 @@
         return [pltpu.make_async_copy(w_hbm.at[:, where(cc, yy, k)], wbuf.at[k, cc, yy], w_sem.at[k, cc * 2 + yy])
                 for cc in range(2) for yy in range(2)]
 
+    inputs = (pltpu.make_async_copy(ov_hbm, ov_ref, in_sem.at[0]), pltpu.make_async_copy(h_hbm, hbuf, in_sem.at[1]))
+    for cp in inputs:
+        cp.start()
     for k in range(chunks):
         for cp in weights(k):
             cp.start()
     nb = ov_ref.shape[0]
+    for cp in inputs:
+        cp.wait()
     ov_rows[...] = ov_ref[...].astype(f32).reshape(ov_rows.shape).astype(bf16)
     meet([core_peer, y_peer] + [seq_of(p, y, c) for p in zs])
 
@@ -547,9 +586,11 @@
     return pl.pallas_call(
         total_kernel,
         out_shape=jax.ShapeDtypeStruct((nb, nq, dim), bf16),
-        in_specs=[vm, hbm, vm],
+        in_specs=[hbm, hbm, hbm],
         out_specs=vm,
         scratch_shapes=[
+            pltpu.VMEM(ov.shape, bf16),
+            pltpu.VMEM(own_h.shape, bf16),
             pltpu.VMEM((n, w_o.shape[0]), bf16),
             pltpu.VMEM((chunks, 2, 2, w_o.shape[0], lanes), bf16),
             pltpu.VMEM((chunks, 2, 2, n, lanes), f32),
@@ -557,10 +598,10 @@
             pltpu.VMEM((chunks, 2, n, lanes), f32),
             pltpu.VMEM((chunks, n, lanes), f32),
             pltpu.VMEM((chunks, 3, n // NZ, lanes), f32),
-            dma((chunks, 4)), one, one, one, one, three, three, three, three, one, one, one, one,
+            dma((2,)), dma((chunks, 4)), one, one, one, one, three, three, three, three, one, one, one, one,
         ],
         compiler_params=pltpu.CompilerParams(
-            collective_id=1, has_side_effects=True, vmem_limit_bytes=40 * 1024 * 1024),
+            collective_id=1, has_side_effects=True, vmem_limit_bytes=64 * 1024 * 1024 - 65536),
         name="total_all",
     )(ov, w_o, own_h)
 

time: 198 us -> 204 us (1.030)
  Pallas kernels: 185 us -> 192 us
    pallas_call x1, Pallas kernels: 36.5 us -> 43.3 us  [total_all(): pl.pallas_call(total_kernel, out_shape=jax.ShapeDtypeStruct((nb, nq, dim)...]
where the time goes in v5:
time: 204 us
  Pallas kernels  192 us (94%)
  matrix products  8.5 us (4%)
  local copies, waits for them, and re-layouts  3.74 us (2%)
    pallas_call x1, Pallas kernels, attend_all(): pl.pallas_call(functools.partial(attend_kernel, score_scale * math.log2(m...  140 us
    pallas_call x1, Pallas kernels, total_all(): pl.pallas_call(total_kernel, out_shape=jax.ShapeDtypeStruct((nb, nq, dim)...  43.3 us
    dot_general x1, matrix products, local_step(): jnp.einsum('bqhk,hkc->bqhc', q_nope, w_uk, preferred_element_type=f32)  8.5 us
    pallas_call x1, Pallas kernels, rope_queries(): pl.pallas_call(rope_kernel, grid=(steps,), out_shape=jax.ShapeDtypeStruct...  7.91 us

profile of v5, /device:TPU:1, one launch (start us, length us, event | category | flops | bytes accessed | tf_op | source)
XLA Modules:
  0.0 203.9 jit_solution(17591833423666977451)
XLA Ops:
  0.0 7.9 %rope_queries.1.r_hbm = bf16[16,16,128]{2,1,0:T(8,128)(2,1)} custom-call(bf16[16,4,7168]{2,1,0:T(4,128)(2,1)} %h_hbm.1, bf16[512,7168]{1,0:T(8,128)(2,1)} %bitcast.19), custom_call_target="tpu_custom_call" | custom-call | tf_op jit(solution)/shard_map/rope_queries/pallas_call | solution.py:449
  7.9 8.5 %fusion.2 = bf16[16,4,8,512]{3,0,1,2:T(8,128)(2,1)S(1)} fusion(bf16[8,128,512]{2,1,0:T(8,128)(2,1)} %param.15, bf16[7168,8,128,1]{2,1,0,3:T(8,128)(2,1)} %bitcast.24, bf16[16,4,7168,1]{2,1,0,3:T(4,128)(2,1)} %bitcast.20), kind=kOutput, calls=%fused_computation.3 | convolution fusion | flops 1006960640 | bytes 17170432 | tf_op jit(solution)/shard_map/bqhk,hkc->bqhc/dot_general | solution.py:615
  16.4 0.3 copy.10
  16.7 0.1 reshape.12
  16.9 0.9 copy.11
  17.8 140.4 %attend_all.1 = (bf16[16,4,1024]{2,1,0:T(4,128)(2,1)}, bf16[4,4,1792]{2,1,0:T(4,128)(2,1)}) custom-call(s32[16]{0:T(128)} %lens.1, bf16[16,8,16,128]{3,2,1,0:T(8,128)(2,1)} %bitcast.22, bf16[16,16,128]{2,1,0:T(8,128)(2,1)} %rope_queries.1.r_hbm, bf16[16,1024,512]{2,1,0:T(8,128)(2,1)} %c_hbm.1, bf16[16,64,1024]{2,1,0:T(8,128)(2,1)} %bitcast.21, ...), custom_call_target="tpu_custom_call" | custom-call | tf_op jit(solution)/shard_map/attend_all/pallas_call | solution.py:386
  158.2 43.3 %total_all.1 = bf16[16,4,7168]{2,1,0:T(4,128)(2,1)} custom-call(bf16[16,4,1024]{2,1,0:T(4,128)(2,1)} %get-tuple-element.7.ov_hbm, bf16[1024,7168]{1,0:T(8,128)(2,1)} %bitcast.18, bf16[4,4,1792]{2,1,0:T(4,128)(2,1)} %get-tuple-element.8.h_hbm), custom_call_target="tpu_custom_call" | custom-call | tf_op jit(solution)/shard_map/total_all/pallas_call | solution.py:586
  201.5 2.4 %copy.26 = bf16[16,4,7168]{2,1,0:T(4,128)(2,1)} copy(bf16[16,4,7168]{2,1,0:T(4,128)(2,1)} %total_all.1) | data formatting | bytes 1835008

commit v6 on v4

--- a/solution.py
+++ b/solution.py
@@ -161,23 +161,27 @@
 
         k = lax.rem(b, slots)
         row_len = lens[b]
-        pos = s * local_len + lax.broadcasted_iota(jnp.int32, (256, local_len), 1)
-        token = lax.rem(lax.broadcasted_iota(jnp.int32, (256, 1), 0), 16) // 8
-        lane = lax.broadcasted_iota(jnp.int32, (256, 128), 1)
+        pos = s * local_len + lax.broadcasted_iota(jnp.int32, (512, local_len), 1)
+        row = lax.broadcasted_iota(jnp.int32, (512, 1), 0)
+        token = (row // 256) * 2 + lax.rem(row, 16) // 8
+        lane = lax.broadcasted_iota(jnp.int32, (512, 128), 1)
+        q = jnp.concatenate(
+            [jnp.concatenate([qbuf[b, :, :, :, hf * 4 + j].reshape(256, 128) for j in range(4)], axis=1) for hf in range(2)], axis=0)
+        both = qbuf[b, :, :, :, 8].reshape(256, 128)
+        qr = jnp.concatenate([both[:, :64], both[:, 64:]], axis=0)
+        sc = lax.dot_general(q, ck[k], (((1,), (1,)), ((), ())), preferred_element_type=f32)
+        sc = sc + jnp.dot(qr, kr[k], preferred_element_type=f32)
+        sc = jnp.where(pos <= row_len + token, sc, MASK_FILL)
+        m = jnp.max(sc, axis=1, keepdims=True)
+        p = jnp.exp2((sc - m) * scale)
+        l = jnp.sum(p, axis=1, keepdims=True)
+        o = jnp.dot(p.astype(bf16), ck[k], preferred_element_type=f32)
+        stat = jnp.where(lane == 0, m * scale, jnp.where(lane == 1, l, 0.0)).T
         for hf in range(2):
-            q = jnp.concatenate([qbuf[b, :, :, :, hf * 4 + j].reshape(256, 128) for j in range(4)], axis=1)
-            qr = qbuf[b, :, :, :, 8].reshape(256, 128)[:, hf * 64:(hf + 1) * 64]
-            sc = lax.dot_general(q, ck[k], (((1,), (1,)), ((), ())), preferred_element_type=f32)
-            sc = sc + jnp.dot(qr, kr[k], preferred_element_type=f32)
-            sc = jnp.where(pos <= row_len + hf * 2 + token, sc, MASK_FILL)
-            m = jnp.max(sc, axis=1, keepdims=True)
-            p = jnp.exp2((sc - m) * scale)
-            l = jnp.sum(p, axis=1, keepdims=True)
-            o = jnp.dot(p.astype(bf16), ck[k], preferred_element_type=f32)
-            o_full[b, :, :, :, hf * 16:(hf + 1) * 16, :] = o.reshape(2, 2, 4, 16, o.shape[1])
-            stat = jnp.where(lane == 0, m * scale, jnp.where(lane == 1, l, 0.0)).T
+            o_full[b, :, :, :, hf * 16:(hf + 1) * 16, :] = o[hf * 256:(hf + 1) * 256].reshape(2, 2, 4, 16, o.shape[1])
             for cc in range(2):
-                ml0[b, cc, hf * 2:hf * 2 + 2, :] = stat[0:2, cc * 128:(cc + 1) * 128]
+                at = hf * 256 + cc * 128
+                ml0[b, cc, hf * 2:hf * 2 + 2, :] = stat[0:2, at:at + 128]
             sum_c(b, hf).start()
         stat_c(b).start()
 
@@ -386,39 +390,32 @@
     )(lens, q, q_rope, c_kv, k_t, hidden, w_uv)
 
 
-def rope_kernel(h_ref, w_ref, out, acc, rows):
-    step = pl.program_id(0)
-    nb, nq, lanes = h_ref.shape
-    h = h_ref[...].astype(f32).reshape(nb * nq, lanes).astype(bf16)
-    part = lax.dot_general(h, w_ref[...], (((1,), (1,)), ((), ())), preferred_element_type=f32)
-
-    @pl.when(step == 0)
+def rope_kernel(h_ref, w_ref, out, flat, rows):
+    head = pl.program_id(0)
+    nb, nq, _ = h_ref.shape
+
+    @pl.when(head == 0)
     def _():
-        acc[...] = part
-
-    @pl.when(step > 0)
+        flat[...] = h_ref[...].astype(f32).reshape(flat.shape).astype(bf16)
+
+    rows[head] = lax.dot_general(flat[...], w_ref[0], (((1,), (1,)), ((), ())), preferred_element_type=f32)
+
+    @pl.when(head == pl.num_programs(0) - 1)
     def _():
-        acc[...] += part
-
-    @pl.when(step == pl.num_programs(0) - 1)
-    def _():
-        for h in range(8):
-            rows[:, h, :] = acc[:, h * 64:(h + 1) * 64]
-        pairs = rows[...].reshape(nb, 2, 16, 64)
+        pairs = jnp.stack([rows[h] for h in range(8)], axis=1).reshape(nb, 2, 16, 64)
         out[...] = jnp.concatenate([pairs[:, 0], pairs[:, 1]], axis=-1).astype(bf16)
 
 
 def rope_queries(hidden, w_t):
     nb, nq, dim = hidden.shape
-    wide = w_t.shape[0]
-    steps = next(k for k in (7, 4, 1) if dim % (k * 128) == 0)
+    heads, wide = w_t.shape[:2]
     return pl.pallas_call(
         rope_kernel,
-        grid=(steps,),
+        grid=(heads,),
         out_shape=jax.ShapeDtypeStruct((nb, 16, 128), bf16),
-        in_specs=[pl.BlockSpec((nb, nq, dim // steps), lambda i: (0, 0, i)), pl.BlockSpec((wide, dim // steps), lambda i: (0, i))],
+        in_specs=[pl.BlockSpec((nb, nq, dim), lambda i: (0, 0, 0)), pl.BlockSpec((1, wide, dim), lambda i: (i, 0, 0))],
         out_specs=pl.BlockSpec((nb, 16, 128), lambda i: (0, 0, 0)),
-        scratch_shapes=[pltpu.VMEM((nb * nq, wide), f32), pltpu.VMEM((nb * nq, 8, 64), f32)],
+        scratch_shapes=[pltpu.VMEM((nb * nq, dim), bf16), pltpu.VMEM((heads, nb * nq, wide), f32)],
         compiler_params=pltpu.CompilerParams(dimension_semantics=("arbitrary",)),
         name="rope_queries",
     )(hidden, w_t)
@@ -573,7 +570,7 @@
         q_nope = jnp.einsum("cre,eil->cril", hidden, w_uq, preferred_element_type=f32).astype(bf16)
         q_lat = jnp.einsum("bqhk,hkc->bqhc", q_nope, w_uk, preferred_element_type=f32).astype(bf16)
         q = q_lat.reshape(nb, 2, 16, 4, 128).transpose(0, 1, 3, 2, 4).reshape(nb, 8, 16, 128)
-        q_rope = rope_queries(hidden, w_qr.transpose(1, 2, 0).reshape(-1, dim))
+        q_rope = rope_queries(hidden, w_qr.transpose(1, 2, 0))
         o_val, own_h = attend_all(q, q_rope, cache_lens, c_kv, jnp.swapaxes(k_r, 1, 2), hidden, w_uv, score_scale)
         return total_all(o_val, w_o.reshape(-1, dim), own_h)
 

time: 198 us -> 197 us (level)
  no operation moved by 1% of the time
where the time goes in v6:
time: 197 us
  Pallas kernels  184 us (93%)
  matrix products  8.5 us (4%)
  local copies, waits for them, and re-layouts  3.96 us (2%)
    pallas_call x1, Pallas kernels, attend_all(): pl.pallas_call(functools.partial(attend_kernel, score_scale * math.log2(m...  140 us
    pallas_call x1, Pallas kernels, total_all(): pl.pallas_call(total_kernel, out_shape=jax.ShapeDtypeStruct((nb, nq, dim)...  36.3 us
    dot_general x1, matrix products, local_step(): jnp.einsum('bqhk,hkc->bqhc', q_nope, w_uk, preferred_element_type=f32)  8.5 us
    pallas_call x1, Pallas kernels, rope_queries(): pl.pallas_call(rope_kernel, grid=(heads,), out_shape=jax.ShapeDtypeStruct...  8.2 us

profile of v6, /device:TPU:1, one launch (start us, length us, event | category | flops | bytes accessed | tf_op | source)
XLA Modules:
  0.0 196.8 jit_solution(9198101167972542835)
XLA Ops:
  0.0 8.2 %rope_queries.1.r_hbm = bf16[16,16,128]{2,1,0:T(8,128)(2,1)} custom-call(bf16[16,4,7168]{2,1,0:T(4,128)(2,1)} %h_hbm.1, bf16[8,64,7168]{2,1,0:T(8,128)(2,1)} %bitcast.17), custom_call_target="tpu_custom_call" | custom-call | tf_op jit(solution)/shard_map/rope_queries/pallas_call | solution.py:412
  8.2 8.5 %fusion.2 = bf16[16,4,8,512]{3,0,1,2:T(8,128)(2,1)S(1)} fusion(bf16[8,128,512]{2,1,0:T(8,128)(2,1)} %param.15, bf16[7168,8,128,1]{2,1,0,3:T(8,128)(2,1)} %bitcast.22, bf16[16,4,7168,1]{2,1,0,3:T(4,128)(2,1)} %bitcast.18), kind=kOutput, calls=%fused_computation.3 | convolution fusion | flops 1006960640 | bytes 17170432 | tf_op jit(solution)/shard_map/bqhk,hkc->bqhc/dot_general | solution.py:571
  16.7 0.3 copy.10
  17.0 0.1 reshape.9
  17.1 0.9 copy.11
  18.0 139.8 %attend_all.1 = (bf16[16,4,1024]{2,1,0:T(4,128)(2,1)}, bf16[4,4,1792]{2,1,0:T(4,128)(2,1)}) custom-call(s32[16]{0:T(128)} %lens.1, bf16[16,8,16,128]{3,2,1,0:T(8,128)(2,1)} %bitcast.20, bf16[16,16,128]{2,1,0:T(8,128)(2,1)} %rope_queries.1.r_hbm, bf16[16,1024,512]{2,1,0:T(8,128)(2,1)} %c_hbm.1, bf16[16,64,1024]{2,1,0:T(8,128)(2,1)} %bitcast.19, ...), custom_call_target="tpu_custom_call" | custom-call | tf_op jit(solution)/shard_map/attend_all/pallas_call | solution.py:356
  157.8 0.0 copy-start
  157.8 0.9 copy-done
  158.7 0.0 copy-start.1
  158.7 0.8 copy-done.1
  159.6 36.3 %total_all.1 = bf16[16,4,7168]{2,1,0:T(4,128)(2,1)S(1)} custom-call(bf16[16,4,1024]{2,1,0:T(4,128)(2,1)S(1)} %copy-done, bf16[1024,7168]{1,0:T(8,128)(2,1)} %bitcast.16, bf16[4,4,1792]{2,1,0:T(4,128)(2,1)S(1)} %copy-done.1), custom_call_target="tpu_custom_call" | custom-call | tf_op jit(solution)/shard_map/total_all/pallas_call | solution.py:544
  195.9 0.9 copy.26
Async XLA Ops:
  157.8 0.9 copy-start
  158.7 0.8 copy-start.1

commit v7 on v6

--- a/solution.py
+++ b/solution.py
@@ -304,10 +304,10 @@
     def _(b):
         gather_y(b, y).start()
 
-    steps = ((7, step_e), (8, functools.partial(step_g, 1)), (9, functools.partial(step_g, 2)), (10, step_f),
-             (0, step_z1), (1, step_z2), (2, step_z3), (3, step_z4), (5, step_d), (4, attend))
-
-    @pl.loop(0, nb + 10)
+    steps = ((8, step_e), (6, step_d), (4, step_z4), (5, attend), (3, step_z3), (12, functools.partial(step_g, 2)),
+             (2, step_z2), (0, step_z1), (14, step_f), (10, functools.partial(step_g, 1)))
+
+    @pl.loop(0, nb + 14)
     def _(it):
         for lag, fn in steps:
             b = it - lag

time: 197 us -> 195 us (0.990)
  Pallas kernels: 184 us -> 182 us
    pallas_call x1, Pallas kernels: 36.3 us -> 33.8 us  [total_all(): pl.pallas_call(total_kernel, out_shape=jax.ShapeDtypeStruct((nb, nq, dim)...]
where the time goes in v7:
time: 195 us; the launch traced here: 194 us
  Pallas kernels  182 us (93%)
  matrix products  8.5 us (4%)
  local copies, waits for them, and re-layouts  3.96 us (2%)
    pallas_call x1, Pallas kernels, attend_all(): pl.pallas_call(functools.partial(attend_kernel, score_scale * math.log2(m...  140 us
    pallas_call x1, Pallas kernels, total_all(): pl.pallas_call(total_kernel, out_shape=jax.ShapeDtypeStruct((nb, nq, dim)...  33.8 us
    dot_general x1, matrix products, local_step(): jnp.einsum('bqhk,hkc->bqhc', q_nope, w_uk, preferred_element_type=f32)  8.5 us
    pallas_call x1, Pallas kernels, rope_queries(): pl.pallas_call(rope_kernel, grid=(heads,), out_shape=jax.ShapeDtypeStruct...  8.2 us

profile of v7, /device:TPU:1, one launch (start us, length us, event | category | flops | bytes accessed | tf_op | source)
XLA Modules:
  0.0 194.2 jit_solution(15190169235512729535)
XLA Ops:
  0.0 8.2 %rope_queries.1.r_hbm = bf16[16,16,128]{2,1,0:T(8,128)(2,1)} custom-call(bf16[16,4,7168]{2,1,0:T(4,128)(2,1)} %h_hbm.1, bf16[8,64,7168]{2,1,0:T(8,128)(2,1)} %bitcast.17), custom_call_target="tpu_custom_call" | custom-call | tf_op jit(solution)/shard_map/rope_queries/pallas_call | solution.py:412
  8.2 8.5 %fusion.2 = bf16[16,4,8,512]{3,0,1,2:T(8,128)(2,1)S(1)} fusion(bf16[8,128,512]{2,1,0:T(8,128)(2,1)} %param.15, bf16[7168,8,128,1]{2,1,0,3:T(8,128)(2,1)} %bitcast.22, bf16[16,4,7168,1]{2,1,0,3:T(4,128)(2,1)} %bitcast.18), kind=kOutput, calls=%fused_computation.3 | convolution fusion | flops 1006960640 | bytes 17170432 | tf_op jit(solution)/shard_map/bqhk,hkc->bqhc/dot_general | solution.py:571
  16.7 0.3 copy.10
  17.0 0.1 reshape.9
  17.1 0.9 copy.11
  18.0 139.7 %attend_all.1 = (bf16[16,4,1024]{2,1,0:T(4,128)(2,1)}, bf16[4,4,1792]{2,1,0:T(4,128)(2,1)}) custom-call(s32[16]{0:T(128)} %lens.1, bf16[16,8,16,128]{3,2,1,0:T(8,128)(2,1)} %bitcast.20, bf16[16,16,128]{2,1,0:T(8,128)(2,1)} %rope_queries.1.r_hbm, bf16[16,1024,512]{2,1,0:T(8,128)(2,1)} %c_hbm.1, bf16[16,64,1024]{2,1,0:T(8,128)(2,1)} %bitcast.19, ...), custom_call_target="tpu_custom_call" | custom-call | tf_op jit(solution)/shard_map/attend_all/pallas_call | solution.py:356
  157.7 0.0 copy-start
  157.7 0.9 copy-done
  158.6 0.0 copy-start.1
  158.6 0.8 copy-done.1
  159.4 33.8 %total_all.1 = bf16[16,4,7168]{2,1,0:T(4,128)(2,1)S(1)} custom-call(bf16[16,4,1024]{2,1,0:T(4,128)(2,1)S(1)} %copy-done, bf16[1024,7168]{1,0:T(8,128)(2,1)} %bitcast.16, bf16[4,4,1792]{2,1,0:T(4,128)(2,1)S(1)} %copy-done.1), custom_call_target="tpu_custom_call" | custom-call | tf_op jit(solution)/shard_map/total_all/pallas_call | solution.py:544
  193.3 0.9 copy.26
Async XLA Ops:
  157.7 0.9 copy-start
  158.6 0.8 copy-start.1

commit v8 on v7

--- a/solution.py
+++ b/solution.py
@@ -9,6 +9,7 @@
 from jax.sharding import PartitionSpec as P
 
 MASK_FILL = -1e30
+ATTEND_VMEM = 46 * 1024 * 1024
 NZ, NY, NC = 4, 2, 2
 MESH = pl.DeviceIdType.MESH
 f32, bf16 = jnp.float32, jnp.bfloat16
@@ -41,14 +42,14 @@
     return jnp.concatenate([rows, pad], axis=0).T
 
 
-def attend_kernel(scale, lens, q_hbm, r_hbm, c_hbm, k_hbm, h_hbm, wuv, out, h_out,
+def attend_kernel(scale, lens, q_hbm, r_hbm, c_hbm, k_hbm, h_hbm, w_hbm, wuv, out, h_out, w_out,
                   qbuf, ck, kr, o_full, ml0, ml1, ml2, rc_c, ml_c, rc_y, ml_y,
                   rc_u, ml_u, ml_us, rc_d, ml_d, ml_ds, wcol,
-                  q_sem, h_sem, c_sem, k_sem,
+                  q_sem, h_sem, w_sem, c_sem, k_sem,
                   ay_s, ay_r, au_s, au_r, ad_s, ad_r, ac_s, ac_r,
                   oc_s, oc_r, oy_s, oy_r, ou_s, ou_r, od_s, od_r,
                   mc_s, mc_r, my_s, my_r, mu_s, mu_r, md_s, md_r):
-    nb, slots = q_hbm.shape[0], ck.shape[0]
+    nb, slots, ring = q_hbm.shape[0], ck.shape[0], rc_c.shape[0]
     local_len = ck.shape[1]
     s, z, y, c = place()
     core_peer, y_peer = seq_of(z, y, 1 - c), seq_of(z, 1 - y, c)
@@ -72,6 +73,8 @@
     own_h = pltpu.make_async_copy(
         h_hbm.at[pl.ds(z * deep, deep), :, pl.ds(pl.multiple_of((c * NY + y) * wide, 128), wide)], h_out, h_sem)
     own_h.start()
+    own_w = pltpu.make_async_copy(w_hbm, w_out, w_sem)
+    own_w.start()
     meet([core_peer, y_peer, upper, lower])
     for cp in own_q:
         cp.wait()
@@ -94,13 +97,13 @@
 
     def sum_c(b, hf):
         rows = pl.ds(hf * 16, 16)
-        return remote(o_full.at[b, 1 - c, :, :, rows], rc_c.at[b, :, :, rows], oc_s.at[b, hf], oc_r.at[b, hf], core_peer)
+        return remote(o_full.at[b, 1 - c, :, :, rows], rc_c.at[lax.rem(b, ring), :, :, rows], oc_s.at[b, hf], oc_r.at[b, hf], core_peer)
 
     def stat_c(b):
         return remote(ml0.at[b, 1 - c], ml_c.at[b], mc_s.at[b], mc_r.at[b], core_peer)
 
     def sum_y(b):
-        return (remote(o_full.at[b, c, 1 - y], rc_y.at[b], oy_s.at[b], oy_r.at[b], y_peer),
+        return (remote(o_full.at[b, c, 1 - y], rc_y.at[lax.rem(b, ring)], oy_s.at[b], oy_r.at[b], y_peer),
                 remote(ml1.at[b], ml_y.at[b], my_s.at[b], my_r.at[b], y_peer))
 
     def sum_up(b, dest, d):
@@ -205,7 +208,7 @@
         for hf in range(2):
             rows = pl.ds(hf * 16, 16)
             wa, wb = (cols[:, 2 * hf + j:2 * hf + j + 1].reshape(2, 4, 16, 1) for j in range(2))
-            o_full[b, c, :, :, rows, :] = o_full[b, c, :, :, rows, :] * wa + rc_c[b, :, :, rows, :] * wb
+            o_full[b, c, :, :, rows, :] = o_full[b, c, :, :, rows, :] * wa + rc_c[lax.rem(b, ring), :, :, rows, :] * wb
         for cp in sum_y(b):
             cp.start()
 
@@ -219,7 +222,7 @@
         for hf in range(2):
             rows = pl.ds(hf * 16, 16)
             wa, wb = (cols[:, 2 * hf + j:2 * hf + j + 1].reshape(4, 16, 1) for j in range(2))
-            o_full[b, c, y, :, rows, :] = o_full[b, c, y, :, rows, :] * wa + rc_y[b, :, rows, :] * wb
+            o_full[b, c, y, :, rows, :] = o_full[b, c, y, :, rows, :] * wa + rc_y[lax.rem(b, ring), :, rows, :] * wb
 
         @pl.when(z == 0)
         def _():
@@ -317,6 +320,7 @@
                 fn(b)
 
     own_h.wait()
+    own_w.wait()
 
     @pl.loop(0, nb)
     def _(b):
@@ -348,18 +352,20 @@
                     stat_down(b, ml2).wait_send()
 
 
-def attend_all(q, q_rope, lens, c_kv, k_t, hidden, w_uv, score_scale):
+def attend_all(q, q_rope, lens, c_kv, k_t, hidden, w_o, w_uv, score_scale):
     nb, local_len, lat = c_kv.shape
     nq, dim = hidden.shape[1:]
     slots = 3
     dma = pltpu.SemaphoreType.DMA
     return pl.pallas_call(
         functools.partial(attend_kernel, score_scale * math.log2(math.e)),
-        out_shape=(jax.ShapeDtypeStruct((nb, nq, w_uv.shape[0] * w_uv.shape[2]), bf16),
-                   jax.ShapeDtypeStruct((nb // NZ, nq, dim // 4), bf16)),
-        in_specs=[pl.BlockSpec(memory_space=pltpu.SMEM)] + [pl.BlockSpec(memory_space=pl.ANY)] * 5
+        out_shape=(pltpu.VMEM((nb, nq, w_uv.shape[0] * w_uv.shape[2]), bf16),
+                   pltpu.VMEM((nb // NZ, nq, dim // 4), bf16),
+                   pltpu.VMEM(w_o.shape, bf16)),
+        in_specs=[pl.BlockSpec(memory_space=pltpu.SMEM)] + [pl.BlockSpec(memory_space=pl.ANY)] * 6
         + [pl.BlockSpec(memory_space=pltpu.VMEM)],
-        out_specs=(pl.BlockSpec(memory_space=pltpu.VMEM), pl.BlockSpec(memory_space=pltpu.VMEM)),
+        out_specs=(pl.BlockSpec(memory_space=pltpu.VMEM), pl.BlockSpec(memory_space=pltpu.VMEM),
+                   pl.BlockSpec(memory_space=pl.ANY)),
         scratch_shapes=[
             pltpu.VMEM((nb, 2, 2, 4, 9, 16, 128), bf16),
             pltpu.VMEM((slots, local_len, lat), bf16),
@@ -368,26 +374,26 @@
             pltpu.VMEM((nb, 2, 8, 128), f32),
             pltpu.VMEM((nb, 8, 128), f32),
             pltpu.VMEM((nb, 8, 128), f32),
-            pltpu.VMEM((nb, 2, 4, 32, lat), f32),
+            pltpu.VMEM((4, 2, 4, 32, lat), f32),
+            pltpu.VMEM((nb, 8, 128), f32),
+            pltpu.VMEM((4, 4, 32, lat), f32),
             pltpu.VMEM((nb, 8, 128), f32),
             pltpu.VMEM((nb, 4, 32, lat), f32),
             pltpu.VMEM((nb, 8, 128), f32),
+            pltpu.VMEM((nb, 8, 128), f32),
             pltpu.VMEM((nb, 4, 32, lat), f32),
             pltpu.VMEM((nb, 8, 128), f32),
             pltpu.VMEM((nb, 8, 128), f32),
-            pltpu.VMEM((nb, 4, 32, lat), f32),
-            pltpu.VMEM((nb, 8, 128), f32),
-            pltpu.VMEM((nb, 8, 128), f32),
             pltpu.VMEM((128, 128), f32),
-            dma((2,)), dma, dma((slots,)), dma((slots,)),
+            dma((2,)), dma, dma, dma((slots,)), dma((slots,)),
             dma((nb,)), dma((nb,)), dma((nb, 3)), dma((nb, 3)), dma((nb, 3)), dma((nb, 3)), dma((nb,)), dma((nb,)),
             dma((nb, 2)), dma((nb, 2)), dma((nb,)), dma((nb,)), dma((nb, 3)), dma((nb, 3)), dma((nb, 3)), dma((nb, 3)),
             dma((nb,)), dma((nb,)), dma((nb,)), dma((nb,)), dma((nb,)), dma((nb,)), dma((nb,)), dma((nb,)),
         ],
         compiler_params=pltpu.CompilerParams(
-            collective_id=0, has_side_effects=True, vmem_limit_bytes=64 * 1024 * 1024 - 65536),
+            collective_id=0, has_side_effects=True, vmem_limit_bytes=ATTEND_VMEM),
         name="attend_all",
-    )(lens, q, q_rope, c_kv, k_t, hidden, w_uv)
+    )(lens, q, q_rope, c_kv, k_t, hidden, w_o, w_uv)
 
 
 def rope_kernel(h_ref, w_ref, out, flat, rows):
@@ -421,10 +427,10 @@
     )(hidden, w_t)
 
 
-def total_kernel(ov_ref, w_hbm, hbuf, out, ov_rows, wbuf, part, gat, rc_c, rc_y, rc_z,
-                 w_sem, sc_s, sc_r, sy_s, sy_r, sz_s, sz_r, gz_s, gz_r, gy_s, gy_r, gc_s, gc_r):
+def total_kernel(ov_ref, w_ref, hbuf, out, ov_rows, part, gat, rc_c, rc_y, rc_z,
+                 sc_s, sc_r, sy_s, sy_r, sz_s, sz_r, gz_s, gz_r, gy_s, gy_r, gc_s, gc_r):
     _, z, y, c = place()
-    chunks, lanes = wbuf.shape[0], wbuf.shape[4]
+    chunks, lanes = part.shape[0], part.shape[4]
     deep = part.shape[3] // NZ
     core_peer, y_peer = seq_of(z, y, 1 - c), seq_of(z, 1 - y, c)
     zs = [lax.rem(z + d, NZ) for d in (1, 2, 3)]
@@ -433,13 +439,6 @@
     def where(cc, yy, k):
         return pl.ds(pl.multiple_of((cc * NY + yy) * (chunks * lanes) + k * lanes, 128), lanes)
 
-    def weights(k):
-        return [pltpu.make_async_copy(w_hbm.at[:, where(cc, yy, k)], wbuf.at[k, cc, yy], w_sem.at[k, cc * 2 + yy])
-                for cc in range(2) for yy in range(2)]
-
-    for k in range(chunks):
-        for cp in weights(k):
-            cp.start()
     nb = ov_ref.shape[0]
     ov_rows[...] = ov_ref[...].astype(f32).reshape(ov_rows.shape).astype(bf16)
     meet([core_peer, y_peer] + [seq_of(p, y, c) for p in zs])
@@ -467,12 +466,10 @@
         return remote(gat.at[k, cc], gat.at[k, cc], gc_s.at[k], gc_r.at[k], core_peer)
 
     def multiply(k):
-        for cp in weights(k):
-            cp.wait()
         ov = ov_rows[...]
         for cc in (1 - c, c):
             for yy in range(2):
-                part[k, cc, yy] = jnp.dot(ov, wbuf[k, cc, yy], preferred_element_type=f32)
+                part[k, cc, yy] = jnp.dot(ov, w_ref[:, where(cc, yy, k)], preferred_element_type=f32)
             if cc is not c:
                 sum_c(k).start()
 
@@ -539,25 +536,24 @@
     chunks = next(k for k in (7, 1) if dim % (4 * k * 128) == 0)
     lanes = dim // (4 * chunks)
     dma = pltpu.SemaphoreType.DMA
-    vm, hbm = pl.BlockSpec(memory_space=pltpu.VMEM), pl.BlockSpec(memory_space=pl.ANY)
+    vm = pl.BlockSpec(memory_space=pltpu.VMEM)
     one, three = dma((chunks,)), dma((chunks, 3))
     return pl.pallas_call(
         total_kernel,
-        out_shape=jax.ShapeDtypeStruct((nb, nq, dim), bf16),
-        in_specs=[vm, hbm, vm],
+        out_shape=pltpu.VMEM((nb, nq, dim), bf16),
+        in_specs=[vm, vm, vm],
         out_specs=vm,
         scratch_shapes=[
             pltpu.VMEM((n, w_o.shape[0]), bf16),
-            pltpu.VMEM((chunks, 2, 2, w_o.shape[0], lanes), bf16),
             pltpu.VMEM((chunks, 2, 2, n, lanes), f32),
             pltpu.VMEM((chunks, 2, 2, n, lanes), bf16),
             pltpu.VMEM((chunks, 2, n, lanes), f32),
             pltpu.VMEM((chunks, n, lanes), f32),
             pltpu.VMEM((chunks, 3, n // NZ, lanes), f32),
-            dma((chunks, 4)), one, one, one, one, three, three, three, three, one, one, one, one,
+            one, one, one, one, three, three, three, three, one, one, one, one,
         ],
         compiler_params=pltpu.CompilerParams(
-            collective_id=1, has_side_effects=True, vmem_limit_bytes=40 * 1024 * 1024),
+            collective_id=1, has_side_effects=True, vmem_limit_bytes=24 * 1024 * 1024),
         name="total_all",
     )(ov, w_o, own_h)
 
@@ -571,8 +567,8 @@
         q_lat = jnp.einsum("bqhk,hkc->bqhc", q_nope, w_uk, preferred_element_type=f32).astype(bf16)
         q = q_lat.reshape(nb, 2, 16, 4, 128).transpose(0, 1, 3, 2, 4).reshape(nb, 8, 16, 128)
         q_rope = rope_queries(hidden, w_qr.transpose(1, 2, 0))
-        o_val, own_h = attend_all(q, q_rope, cache_lens, c_kv, jnp.swapaxes(k_r, 1, 2), hidden, w_uv, score_scale)
-        return total_all(o_val, w_o.reshape(-1, dim), own_h)
+        o_val, own_h, own_w = attend_all(q, q_rope, cache_lens, c_kv, jnp.swapaxes(k_r, 1, 2), hidden, w_o.reshape(-1, dim), w_uv, score_scale)
+        return total_all(*(pltpu.with_memory_space_constraint(v, pltpu.VMEM) for v in (o_val, own_w, own_h)))
 
     specs_in = (P("batch", None, None), P("batch"), P("batch", "seq", None), P("batch", "seq", None),
                 P(None, "seq", None), P(None, "seq", None), P("seq", None, None), P("seq", None, None),

time: 195 us -> 192 us (0.985)
  no operation moved by 1% of the time
where the time goes in v8:
time: 192 us
  Pallas kernels  181 us (94%)
  matrix products  8.31 us (4%)
  local copies, waits for them, and re-layouts  2.24 us (1%)
    pallas_call x1, Pallas kernels, attend_all(): pl.pallas_call(functools.partial(attend_kernel, score_scale * math.log2(m...  139 us
    pallas_call x1, Pallas kernels, total_all(): pl.pallas_call(total_kernel, out_shape=pltpu.VMEM((nb, nq, dim), bf16), i...  33.6 us
    dot_general x1, matrix products, local_step(): jnp.einsum('bqhk,hkc->bqhc', q_nope, w_uk, preferred_element_type=f32)  8.31 us
    pallas_call x1, Pallas kernels, rope_queries(): pl.pallas_call(rope_kernel, grid=(heads,), out_shape=jax.ShapeDtypeStruct...  8.28 us

profile of v8, /device:TPU:1, one launch (start us, length us, event | category | flops | bytes accessed | tf_op | source)
XLA Modules:
  0.0 191.6 jit_solution(1387109553118093085)
XLA Ops:
  0.0 0.0 copy-start
  0.0 8.3 %rope_queries.1.r_hbm = bf16[16,16,128]{2,1,0:T(8,128)(2,1)} custom-call(bf16[16,4,7168]{2,1,0:T(4,128)(2,1)} %h_hbm.1, bf16[8,64,7168]{2,1,0:T(8,128)(2,1)} %bitcast.17), custom_call_target="tpu_custom_call" | custom-call | tf_op jit(solution)/shard_map/rope_queries/pallas_call | solution.py:418
  8.3 0.0 copy-done
  8.3 8.3 %fusion.2 = bf16[16,4,8,512]{3,0,1,2:T(8,128)(2,1)S(1)} fusion(bf16[8,128,512]{2,1,0:T(8,128)(2,1)S(1)} %copy-done, bf16[7168,8,128,1]{2,1,0,3:T(8,128)(2,1)} %bitcast.22, bf16[16,4,7168,1]{2,1,0,3:T(4,128)(2,1)} %bitcast.18), kind=kOutput, calls=%fused_computation.3 | convolution fusion | flops 1006960640 | bytes 17170432 | tf_op jit(solution)/shard_map/bqhk,hkc->bqhc/dot_general | solution.py:567
  16.6 0.3 copy.10
  16.9 0.1 reshape.9
  17.0 0.9 copy.11
  17.9 0.0 copy-start.1
  17.9 139.1 %attend_all.1 = (bf16[16,4,1024]{2,1,0:T(4,128)(2,1)S(1)}, bf16[4,4,1792]{2,1,0:T(4,128)(2,1)S(1)}, bf16[1024,7168]{1,0:T(8,128)(2,1)S(1)}) custom-call(s32[16]{0:T(128)} %lens.1, bf16[16,8,16,128]{3,2,1,0:T(8,128)(2,1)} %bitcast.19, bf16[16,16,128]{2,1,0:T(8,128)(2,1)} %rope_queries.1.r_hbm, bf16[16,1024,512]{2,1,0:T(8,128)(2,1)} %c_hbm.1, ...), custom_call_target="tpu_custom_call" | custom-call | tf_op jit(solution)/shard_map/attend_all/pallas_call | solution.py:360
  157.0 33.6 %total_all.1 = bf16[16,4,7168]{2,1,0:T(4,128)(2,1)S(1)} custom-call(bf16[16,4,1024]{2,1,0:T(4,128)(2,1)S(1)} %get-tuple-element.8.ov_ref, bf16[1024,7168]{1,0:T(8,128)(2,1)S(1)} %get-tuple-element.9.w_ref, bf16[4,4,1792]{2,1,0:T(4,128)(2,1)S(1)} %get-tuple-element.10.hbuf), custom_call_target="tpu_custom_call" | custom-call | tf_op jit(solution)/shard_map/total_all/pallas_call | solution.py:541
  190.6 0.9 copy.26
  191.6 0.0 copy-done.1
Async XLA Ops:
  0.0 8.3 %copy-start = (bf16[8,128,512]{2,1,0:T(8,128)(2,1)S(1)}, bf16[8,128,512]{2,1,0:T(8,128)(2,1)}, u32[]{:S(2)}) copy-start(bf16[8,128,512]{2,1,0:T(8,128)(2,1)} %param.15) | copy-start | bytes 3145732
  17.9 173.6 %copy-start.1 = (bf16[8,128,512]{2,1,0:T(8,128)(2,1)S(1)}, bf16[8,128,512]{2,1,0:T(8,128)(2,1)}, u32[]{:S(2)}) copy-start(bf16[8,128,512]{2,1,0:T(8,128)(2,1)} %param.15) | copy-start | bytes 3145732

commit v9 on v8

--- a/solution.py
+++ b/solution.py
@@ -508,9 +508,9 @@
             for yy in range(2):
                 out[:, :, where(cc, yy, k)] = gat[k, cc, yy].astype(f32).reshape(nb, -1, lanes).astype(bf16)
 
-    steps = ((10, step_j), (9, step_i), (7, step_h), (5, step_f), (3, step_e), (1, step_d), (0, multiply))
-
-    @pl.loop(0, chunks + 10)
+    steps = ((4, step_e), (12, step_h), (15, step_i), (0, multiply), (1, step_d), (17, step_j), (7, step_f))
+
+    @pl.loop(0, chunks + 17)
     def _(it):
         for lag, fn in steps:
             k = it - lag

time: 192 us -> 191 us (level)
  no operation moved by 1% of the time
where the time goes in v9:
time: 191 us
  Pallas kernels  180 us (94%)
  matrix products  8.31 us (4%)
  local copies, waits for them, and re-layouts  2.24 us (1%)
    pallas_call x1, Pallas kernels, attend_all(): pl.pallas_call(functools.partial(attend_kernel, score_scale * math.log2(m...  139 us
    pallas_call x1, Pallas kernels, total_all(): pl.pallas_call(total_kernel, out_shape=pltpu.VMEM((nb, nq, dim), bf16), i...  32.9 us
    dot_general x1, matrix products, local_step(): jnp.einsum('bqhk,hkc->bqhc', q_nope, w_uk, preferred_element_type=f32)  8.31 us
    pallas_call x1, Pallas kernels, rope_queries(): pl.pallas_call(rope_kernel, grid=(heads,), out_shape=jax.ShapeDtypeStruct...  8.28 us

profile of v9, /device:TPU:1, one launch (start us, length us, event | category | flops | bytes accessed | tf_op | source)
XLA Modules:
  0.0 190.8 jit_solution(1454465045780129730)
XLA Ops:
  0.0 0.0 copy-start
  0.0 8.3 %rope_queries.1.r_hbm = bf16[16,16,128]{2,1,0:T(8,128)(2,1)} custom-call(bf16[16,4,7168]{2,1,0:T(4,128)(2,1)} %h_hbm.1, bf16[8,64,7168]{2,1,0:T(8,128)(2,1)} %bitcast.17), custom_call_target="tpu_custom_call" | custom-call | tf_op jit(solution)/shard_map/rope_queries/pallas_call | solution.py:418
  8.3 0.0 copy-done
  8.3 8.3 %fusion.2 = bf16[16,4,8,512]{3,0,1,2:T(8,128)(2,1)S(1)} fusion(bf16[8,128,512]{2,1,0:T(8,128)(2,1)S(1)} %copy-done, bf16[7168,8,128,1]{2,1,0,3:T(8,128)(2,1)} %bitcast.22, bf16[16,4,7168,1]{2,1,0,3:T(4,128)(2,1)} %bitcast.18), kind=kOutput, calls=%fused_computation.3 | convolution fusion | flops 1006960640 | bytes 17170432 | tf_op jit(solution)/shard_map/bqhk,hkc->bqhc/dot_general | solution.py:567
  16.6 0.3 copy.10
  16.9 0.1 reshape.9
  17.0 0.9 copy.11
  17.9 0.0 copy-start.1
  17.9 139.1 %attend_all.1 = (bf16[16,4,1024]{2,1,0:T(4,128)(2,1)S(1)}, bf16[4,4,1792]{2,1,0:T(4,128)(2,1)S(1)}, bf16[1024,7168]{1,0:T(8,128)(2,1)S(1)}) custom-call(s32[16]{0:T(128)} %lens.1, bf16[16,8,16,128]{3,2,1,0:T(8,128)(2,1)} %bitcast.19, bf16[16,16,128]{2,1,0:T(8,128)(2,1)} %rope_queries.1.r_hbm, bf16[16,1024,512]{2,1,0:T(8,128)(2,1)} %c_hbm.1, ...), custom_call_target="tpu_custom_call" | custom-call | tf_op jit(solution)/shard_map/attend_all/pallas_call | solution.py:360
  157.0 32.9 %total_all.1 = bf16[16,4,7168]{2,1,0:T(4,128)(2,1)S(1)} custom-call(bf16[16,4,1024]{2,1,0:T(4,128)(2,1)S(1)} %get-tuple-element.8.ov_ref, bf16[1024,7168]{1,0:T(8,128)(2,1)S(1)} %get-tuple-element.9.w_ref, bf16[4,4,1792]{2,1,0:T(4,128)(2,1)S(1)} %get-tuple-element.10.hbuf), custom_call_target="tpu_custom_call" | custom-call | tf_op jit(solution)/shard_map/total_all/pallas_call | solution.py:541
  189.9 0.9 copy.26
  190.8 0.0 copy-done.1
Async XLA Ops:
  0.0 8.3 %copy-start = (bf16[8,128,512]{2,1,0:T(8,128)(2,1)S(1)}, bf16[8,128,512]{2,1,0:T(8,128)(2,1)}, u32[]{:S(2)}) copy-start(bf16[8,128,512]{2,1,0:T(8,128)(2,1)} %param.15) | copy-start | bytes 3145732
  17.9 172.9 %copy-start.1 = (bf16[8,128,512]{2,1,0:T(8,128)(2,1)S(1)}, bf16[8,128,512]{2,1,0:T(8,128)(2,1)}, u32[]{:S(2)}) copy-start(bf16[8,128,512]{2,1,0:T(8,128)(2,1)} %param.15) | copy-start | bytes 3145732
